TPU v7x, 128 devices: a whole 4x4x4 slice. The times are simulated.
128 devices in a mesh: grp: 4 (over y_hi, core), dev: 32 (over x, z, y_lo).
Axes of the slice: x: 4, y: 4 (y_hi: 2, y_lo: 2; y = y_hi * 2 + y_lo), z: 4, core: 2. Of those that a mesh axis runs over, the one named last changes fastest.
Arguments:
- embeddings: bfloat16 [32768, 768], P(('grp', 'dev')), may hold values from -6 to 6
- language: int32 [32768], P(('grp', 'dev')), may hold values from 0 to 108
- sentence_group: int32 [32768], P(('grp', 'dev')), may hold values from 0 to 8191
- pair_mask: int32 [109, 109], replicated, may hold values 0 or 1
Outputs:
- gradient: float32 [32768, 768], P(('grp', 'dev'))
All inputs are finite; a program needn't handle non-finite values.
Results may differ from a plain program's by a relative error of at most 0.0012.
Values may be sent and summed in bfloat16 or wider, within the bound.
No kernel may reach another device: no remote copies, remote signals or barrier semaphores. Data moves between devices by JAX's collectives and lax.ppermute only.
A program may use at most 256 MiB of HBM per device.

v0:
```python
import math

import jax
import jax.numpy as jnp
from jax import lax
from jax.sharding import PartitionSpec as P


def language_onehot(labels_lang, lang_count):
    return (labels_lang[..., None] == jnp.arange(lang_count, dtype=jnp.int32)).astype(jnp.float32)


def coefficients(scores, packed_a, packed_b, weight_table, scale):
    lang_count = weight_table.shape[0]
    onehot_a = language_onehot(packed_a % lang_count, lang_count)
    second_language_indicator = language_onehot(packed_b % lang_count, lang_count)
    group_a = packed_a // lang_count
    group_b = packed_b // lang_count
    weight_applied_terms = jnp.einsum(
        "prl,lm->prm", onehot_a, weight_table, precision=lax.Precision.HIGHEST
    )
    weight_values = jnp.einsum(
        "auk,ack->auc",
        weight_applied_terms,
        second_language_indicator,
        precision=lax.Precision.HIGHEST,
    )
    labels = jnp.where(group_a[:, :, None] == group_b[:, None, :], 1.0, -1.0).astype(jnp.float32)
    return -weight_values * labels * jax.nn.sigmoid(-labels * scores) * scale


def on_device(embeddings, language, sentence_group, pair_mask):
    rows, width = embeddings.shape
    scale = 1.0 / math.sqrt(width)
    lang_count = pair_mask.shape[0]
    weight_table = (pair_mask + pair_mask.T).astype(jnp.float32) * 0.5
    meta = sentence_group * lang_count + language
    device = lax.axis_index(("grp", "dev"))
    own_index = device * rows + jnp.arange(rows, dtype=jnp.int32)

    def piece_terms(piece_rows, piece_meta, start):
        count = piece_rows.shape[0]
        scores = jnp.dot(embeddings, piece_rows.T, preferred_element_type=jnp.float32)[None] * scale
        coef = coefficients(scores, meta[None], piece_meta[None], weight_table, scale)[0]
        column_index = start + jnp.arange(count, dtype=jnp.int32)
        offdiag = (own_index[:, None] != column_index[None, :]).astype(jnp.float32)
        coef = (coef * offdiag).astype(jnp.bfloat16)
        return jnp.dot(coef, piece_rows, preferred_element_type=jnp.float32)

    empty = jnp.zeros((rows, width), jnp.float32)
    total_grad = empty
    piece_rows = lax.all_gather(embeddings, ("grp", "dev"), axis=0, tiled=True)
    piece_meta = lax.all_gather(meta, ("grp", "dev"), axis=0, tiled=True)
    count = piece_rows.shape[0]
    block_rows = 2048
    split_rows = piece_rows.reshape(count // block_rows, block_rows, width)
    split_meta = piece_meta.reshape(count // block_rows, block_rows)

    def scan_block(carry, inputs):
        block_index, block_data, block_meta = inputs
        return (carry + piece_terms(block_data, block_meta, block_index * block_rows), None)

    indices = jnp.arange(count // block_rows, dtype=jnp.int32)
    total_grad, _ = lax.scan(scan_block, total_grad, (indices, split_rows, split_meta))
    return total_grad


def solution(mesh):
    return jax.shard_map(
        on_device,
        mesh=mesh,
        in_specs=(P(("grp", "dev"), None), P(("grp", "dev")), P(("grp", "dev")), P()),
        out_specs=P(("grp", "dev"), None),
        check_vma=False,
    )
```

profile of v0, /device:TPU:1, one launch (start us, length us, event | category | flops | bytes accessed | tf_op | source)
XLA Modules:
  0.0 534.6 jit_solution(4666204534253807057)
XLA Ops:
  6.5 0.7 all-gather.3.cloned.1.call-update
  7.3 0.7 fusion.43
  8.0 281.5 %all-gather = s32[128,1,256]{2,1,0:T(1,128)S(1)} all-gather(s32[1,1,256]{2,1,0:T(1,128)S(1)} %bitcast.72), channel_id=1, replica_groups=mesh['grp'=4,'dev'=32] {'grp','dev'}, dimensions={0}, use_global_device_ids=true | all-gather | bytes 132096 | tf_op jit(solution)/shard_map/all_gather | solution.py:53
  289.8 0.9 copy.6
  290.8 0.8 fusion.42
  291.6 84.1 %all-gather.3.cloned.1.call-done = bf16[32768,768]{1,0:T(8,128)(2,1)} async-done(((bf16[256,768]{1,0:T(8,128)(2,1)}), bf16[32768,768]{1,0:T(8,128)(2,1)}) %all-gather.3.cloned.1.call-update) | async-done | bytes 50331664 | tf_op jit(solution)/shard_map/all_gather | solution.py:52
  375.7 151.2 %while.14 = (s32[]{:T(128)}, f32[256,768]{1,0:T(8,128)S(1)}, s32[16]{0:T(128)S(1)}, s32[256]{0:T(256)S(1)}, f32[109,109]{1,0:T(8,128)S(1)}, /*index=5*/s32[16,20...) while((s32[]{:T(128)}, f32[256,768]{1,0:T(8,128)S(1)}, ...), condition=%wide.region_1.2_spmd.clone, body=%wide.region_0.1_spmd.clone.sunk | while | flops 2342466816 | bytes 14896207 | solution.py:64
  375.8 3.1 fusion.64
  378.9 0.6 dynamic_slice.60
  380.4 1.6 fusion.66
  382.0 3.1 fusion.67
  385.2 3.1 fusion.64
  388.3 0.6 dynamic_slice.60
  389.9 1.6 fusion.66
  391.4 3.1 fusion.67
  394.7 3.1 fusion.64
  399.3 1.6 fusion.66
  400.9 3.1 fusion.67
  404.1 3.1 fusion.64
  407.2 0.6 dynamic_slice.60
  408.8 1.6 fusion.66
  410.4 3.1 fusion.67
  413.6 3.1 fusion.64
  418.2 1.6 fusion.66
  419.8 3.1 fusion.67
  423.1 3.1 fusion.64
  426.2 0.6 dynamic_slice.60
  427.7 1.6 fusion.66
  429.3 3.1 fusion.67
  432.5 3.1 fusion.64
  435.6 0.6 dynamic_slice.60
  437.1 1.6 fusion.66
  438.7 3.1 fusion.67
  442.0 3.1 fusion.64
  445.1 0.6 dynamic_slice.60
  446.6 1.6 fusion.66
  448.2 3.1 fusion.67
  451.4 3.1 fusion.64
  454.5 0.6 dynamic_slice.60
  456.0 1.6 fusion.66
  457.6 3.1 fusion.67
  460.9 3.1 fusion.64
  464.0 0.6 dynamic_slice.60
  465.5 1.6 fusion.66
  467.1 3.1 fusion.67
  470.3 3.1 fusion.64
  474.9 1.6 fusion.66
  476.5 3.1 fusion.67
  479.8 3.1 fusion.64
  484.4 1.6 fusion.66
  486.0 3.1 fusion.67
  489.2 3.1 fusion.64
  493.8 1.6 fusion.66
  495.4 3.1 fusion.67
  498.7 3.1 fusion.64
  503.3 1.6 fusion.66
  504.9 3.1 fusion.67
  508.1 3.1 fusion.64
  512.8 1.6 fusion.66
  514.3 3.1 fusion.67
  517.6 3.1 fusion.64
  522.2 1.6 fusion.66
  523.8 3.1 fusion.67
  526.9 0.9 copy-done
  (94 shorter events, 11.4 us)
Async XLA Ops:
  6.5 369.1 %all-gather.3.cloned.1.call-start = ((), (), s32[]{:S(2)}) async-start(), calls=%async_computation | async-start | bytes 50724864 | tf_op jit(solution)/shard_map/all_gather | solution.py:52
  526.9 0.9 copy-start
Sparse Core Ops, SparseCore 0:
  9.0 366.5 all-gather.2
where the time goes:
time: 536 us; the launch traced here: 535 us
  blocking collectives  281 us (52%)
  matrix products  128 us (24%)
  waiting for transfers between devices  84.8 us (16%)
  between operations  13.4 us (2%)
  local copies, waits for them, and re-layouts  11.6 us (2%)
  loops' own time  11.2 us (2%)
    all_gather x1, blocking collectives, on_device(): piece_meta = lax.all_gather(meta, ('grp', 'dev'), axis=0, tiled=True)  281 us
    all_gather x1, waiting for transfers between devices, on_device(): piece_rows = lax.all_gather(embeddings, ('grp', 'dev'), axis=0, tiled=True)  84.1 us
    dot_general x16, matrix products, piece_terms(): return jnp.dot(coef, piece_rows, preferred_element_type=jnp.float32)  49.5 us
    dot_general x16, matrix products, piece_terms(): jnp.dot(embeddings, piece_rows.T, preferred_element_type=jnp.float32)[None]  49.5 us
    dot_general x16, matrix products, coefficients(): jnp.einsum('auk,ack->auc', weight_applied_terms, second_language_indicato...  25.1 us
    another operation x1, loops' own time, on_device(): lax.scan(scan_block, total_grad, (indices, split_rows, split_meta))  11.2 us
  transfers between devices with their start and end apart: 1, of which 1 were waited for; matrix products, arithmetic and copies ran while one was open for 1% of the time, Pallas kernels for 0%

commit v1 on v0

v1 whole, which is shorter than its diff:
```python
import functools
import math

import jax
import jax.numpy as jnp
from jax import lax
from jax.experimental import pallas as pl
from jax.experimental.pallas import tpu as pltpu
from jax.sharding import PartitionSpec as P


AXES = ("grp", "dev")
NT = (((1,), (1,)), ((), ()))
NN = (((1,), (0,)), ((), ()))
TN = (((0,), (0,)), ((), ()))
LANES = 128
LINK_SCALE = 16.0
BLOCK = 256
META = 16


def position(x, z, y, core):
    return ((y >> 1) * 2 + core) * 32 + x * 8 + z * 2 + (y & 1)


def exchange(value, step):
    pairs = []
    for x in range(4):
        for z in range(4):
            for y in range(4):
                for core in range(2):
                    dx, dz, dy, dc = step(core)
                    pairs.append((position(x, z, y, core), position(x ^ dx, z ^ dz, y ^ dy, core ^ dc)))
    return lax.ppermute(value, AXES, pairs)


PLANE = ((1, 0, 0, 0), (0, 1, 0, 0), (3, 0, 0, 0), (0, 3, 0, 0))
LINE = ((0, 0, 1, 0), (0, 0, 3, 0))


def plane_step(stream, k):
    return lambda core: PLANE[(k + 2 * stream + core) % 4]


def line_step(k):
    return lambda core: LINE[(k + core) % 2]


def partner(core):
    return (0, 0, 0, 1)


def meta_rows(language, group, width):
    row = jnp.concatenate([language, group // LANES, group % LANES]).astype(jnp.bfloat16)
    return jnp.pad(row[None], ((0, META - 1), (0, width - row.shape[0])))


def in_vmem(count):
    return [pl.BlockSpec(memory_space=pltpu.VMEM)] * count


def prepare_body(line_ref, table_ref, weight_ref, group_ref):
    lang_ids = lax.broadcasted_iota(jnp.int32, (LANES, BLOCK), 0).astype(jnp.float32)
    for b in range(4):
        meta = line_ref[b * (BLOCK + META) + BLOCK:(b + 1) * (BLOCK + META), :].astype(jnp.float32)
        row = meta[:1]
        onehot = jnp.where(lang_ids == row[:, :BLOCK], 1.0, 0.0).astype(jnp.bfloat16)
        weights = lax.dot_general(onehot, table_ref[...], TN, preferred_element_type=jnp.float32)
        weight_ref[b * BLOCK:(b + 1) * BLOCK, :] = weights.astype(jnp.bfloat16)
        group = row[:, BLOCK:2 * BLOCK] * 128.0 + row[:, 2 * BLOCK:3 * BLOCK]
        group_ref[b * BLOCK:(b + 1) * BLOCK, :] = jnp.broadcast_to(group, (LANES, BLOCK)).T


def prepare(lines, table):
    return pl.pallas_call(
        prepare_body,
        in_specs=in_vmem(2),
        out_specs=in_vmem(2),
        out_shape=[
            jax.ShapeDtypeStruct((4 * BLOCK, LANES), jnp.bfloat16),
            jax.ShapeDtypeStruct((4 * BLOCK, LANES), jnp.float32),
        ],
        cost_estimate=pl.CostEstimate(flops=2 * 4 * BLOCK * LANES * LANES * 16, transcendentals=0, bytes_accessed=0),
        name="prepare",
    )(lines, table)


def pair_body(units, first, blocks, start, tile, scale, diagonal, has_carry, *refs):
    weight_ref, group_ref, line_ref = refs[:3]
    columns = refs[3:3 + len(units)]
    carry_ref = refs[-2] if has_carry else None
    out_ref = refs[-1]
    log_scale = scale * math.log2(math.e)
    lang_ids = lax.broadcasted_iota(jnp.int32, (LANES, LANES), 0).astype(jnp.float32)
    pitch = LANES + META

    def one_block(i, _):
        b = first + i
        rows = line_ref[pl.ds(pl.multiple_of(b * (BLOCK + META), META), BLOCK), :]
        at = pl.ds(pl.multiple_of(b * BLOCK, BLOCK), BLOCK)
        table_rows = weight_ref[at, :]
        groups = group_ref[at, :]
        total = carry_ref[pl.ds(pl.multiple_of((b - start) * BLOCK, BLOCK), BLOCK), :] if has_carry else None
        for side, (data_ref, count) in enumerate(zip(columns, units)):
            for t in range(0, count, tile):
                pieces = range(t, t + tile)
                data = jnp.concatenate([data_ref[p * pitch:p * pitch + LANES, :] for p in pieces], axis=0)
                metas = [data_ref[p * pitch + LANES:(p + 1) * pitch, :].astype(jnp.float32)[:1] for p in pieces]
                scores = lax.dot_general(rows, data, NT, preferred_element_type=jnp.float32)
                onehots = [jnp.where(lang_ids == m[:, :LANES], 1.0, 0.0).astype(jnp.bfloat16) for m in metas]
                weights = lax.dot_general(
                    table_rows, jnp.concatenate(onehots, axis=1), NN, preferred_element_type=jnp.float32
                )
                coefs = []
                for n, (p, m) in enumerate(zip(pieces, metas)):
                    same = groups == m[:, LANES:2 * LANES] * 128.0 + m[:, 2 * LANES:3 * LANES]
                    span = slice(n * LANES, (n + 1) * LANES)
                    power = jnp.exp2(scores[:, span] * jnp.where(same, log_scale, -log_scale))
                    coef = (weights[:, span] * jnp.where(same, -scale, scale)) * (1.0 / (1.0 + power))
                    if diagonal and p == 0:
                        row = lax.broadcasted_iota(jnp.int32, (BLOCK, LANES), 0) + b * BLOCK
                        column = lax.broadcasted_iota(jnp.int32, (BLOCK, LANES), 1) + side * LANES
                        coef = jnp.where(row == column, 0.0, coef)
                    coefs.append(coef.astype(jnp.bfloat16))
                part = lax.dot_general(
                    jnp.concatenate(coefs, axis=1), data, NN, preferred_element_type=jnp.float32
                )
                total = part if total is None else total + part
        out_ref[pl.ds(pl.multiple_of(i * BLOCK, BLOCK), BLOCK), :] = total
        return 0

    if blocks == 1:
        one_block(0, 0)
    else:
        lax.fori_loop(0, blocks, one_block, 0)


def pairs(weight, group, lines, columns, carry, first, blocks, scale, diagonal=False, tile=4):
    width = lines.shape[1]
    units = [c.shape[0] // (LANES + META) for c in columns]
    start, operands = 0, [weight, group, lines, *columns]
    if carry is not None:
        start, value = carry
        operands.append(value)
    rows, total = BLOCK * blocks, LANES * sum(units)
    return pl.pallas_call(
        functools.partial(pair_body, units, first, blocks, start, tile, scale, diagonal, carry is not None),
        in_specs=in_vmem(len(operands)),
        out_specs=in_vmem(1)[0],
        out_shape=jax.ShapeDtypeStruct((rows, width), jnp.float32),
        input_output_aliases={len(operands) - 1: 0} if carry is not None and value.shape[0] == rows else {},
        compiler_params=pltpu.CompilerParams(vmem_limit_bytes=24 << 20),
        cost_estimate=pl.CostEstimate(
            flops=4 * rows * total * width, transcendentals=2 * rows * total, bytes_accessed=0
        ),
        name="pairs",
    )(*operands)


def to_link(value):
    return (value * LINK_SCALE).astype(jnp.float16)


def from_link(value):
    return value.astype(jnp.float32) * (1.0 / LINK_SCALE)


def join(*values):
    return lax.optimization_barrier(jnp.concatenate(values, axis=0))


def gradient(embeddings, language, sentence_group, pair_mask):
    width = embeddings.shape[1]
    scale = 1.0 / math.sqrt(width)
    lang_count = pair_mask.shape[0]
    table = ((pair_mask + pair_mask.T).astype(jnp.float32) * 0.5).astype(jnp.bfloat16)
    table = jnp.pad(table, ((0, LANES - lang_count), (0, LANES - lang_count)))

    streams = []
    for s in range(2):
        half = slice(s * LANES, (s + 1) * LANES)
        streams.append(join(embeddings[half], meta_rows(language[half], sentence_group[half], width)))
    lines = join(embeddings, meta_rows(language, sentence_group, width))
    parts = []
    for k in range(4):
        if k < 2:
            lines = join(lines, exchange(lines, line_step(k)))
        got = [exchange(streams[s], plane_step(s, k)) for s in range(2)]
        if k < 3:
            streams = [join(a, b) for a, b in zip(streams, got)]
        if k > 0:
            parts.append(streams if k == 1 else got)
    weight, group = prepare(lines, table)
    others = [[exchange(join(*part), partner)] for part in parts]

    def step(*rest, **options):
        return pairs(weight, group, lines, *rest, scale=scale, **options)

    total = step(parts[0], None, 0, 4, diagonal=True)
    total = step(others[0], (0, total), 0, 4)
    total = step(parts[1], (0, total), 0, 4)
    total = step(others[1], (0, total), 0, 4)
    late = step(parts[2], (0, total), 2, 2)
    far = step(others[2], (2, late), 3, 1)
    relay = exchange(to_link(far), line_step(0))
    near0 = step(parts[2] + others[2], (0, total), 1, 1)
    back0 = exchange(to_link(near0), line_step(0))
    near1 = step(others[2], (2, late), 2, 1)
    back1 = exchange(to_link(near1 + from_link(relay)), line_step(1))
    final = step(parts[2] + others[2], (0, total), 0, 1)
    return final + from_link(back0) + from_link(back1)


def solution(mesh):
    return jax.shard_map(
        gradient,
        mesh=mesh,
        in_specs=(P(AXES, None), P(AXES), P(AXES), P()),
        out_specs=P(AXES, None),
        check_vma=False,
    )
```

time: 536 us -> 153 us (0.29)
  blocking collectives: 281 us -> 0 us
  matrix products: 128 us -> 0 us
  Pallas kernels: 0 us -> 44.9 us
  starting transfers between devices: 0.01 us -> 28.9 us
  waiting for transfers between devices: 84.8 us -> 57.5 us
  between operations: 13.4 us -> 0.37 us
  loops' own time: 11.2 us -> 0 us
  other arithmetic: 3.92 us -> 11.9 us
    all_gather x1 -> x0, blocking collectives: 281 us -> none  [on_device(): piece_meta = lax.all_gather(meta, ('grp', 'dev'), axis=0, tiled=True)]
    dot_general x64 -> x0, matrix products: 128 us -> none  [the longest x16 49.5 us: piece_terms(): return jnp.dot(coef, piece_rows, preferred_element_type=jnp.float32)]
    all_gather x1 -> x0, waiting for transfers between devices: 84.1 us -> none  [on_device(): piece_rows = lax.all_gather(embeddings, ('grp', 'dev'), axis=0, tiled=True)]
    ppermute x0 -> x16, waiting for transfers between devices: none -> 57.5 us  [exchange(): return lax.ppermute(value, AXES, pairs)]
    pallas_call x0 -> x10, Pallas kernels: none -> 44.9 us  [the longest x9 42.3 us: pairs(): pl.pallas_call(functools.partial(pair_body, units, first, blocks, start,...]
    ppermute x0 -> x16, starting transfers between devices: none -> 28.9 us  [exchange(): return lax.ppermute(value, AXES, pairs)]
    another operation x1 -> x0, loops' own time: 11.2 us -> none  [on_device(): lax.scan(scan_block, total_grad, (indices, split_rows, split_meta))]
    dynamic_slice x16 -> x0, local copies, waits for them, and re-layouts: 9.78 us -> none  [on_device(): lax.scan(scan_block, total_grad, (indices, split_rows, split_meta))]
  transfers between devices with their start and end apart: 1 -> 16, of which waited for: 1 -> 12; matrix products, arithmetic and copies ran while one was open for 1% -> 5% of each run, Pallas kernels for 0% -> 28%
where the time goes in v1:
time: 153 us
  waiting for transfers between devices  57.5 us (38%)
  Pallas kernels  44.9 us (29%)
  starting transfers between devices  28.9 us (19%)
  other arithmetic  11.9 us (8%)
  local copies, waits for them, and re-layouts  9.22 us (6%)
    ppermute x16, waiting for transfers between devices, exchange(): return lax.ppermute(value, AXES, pairs)  57.5 us
    pallas_call x9, Pallas kernels, pairs(): pl.pallas_call(functools.partial(pair_body, units, first, blocks, start,...  42.3 us
    ppermute x16, starting transfers between devices, exchange(): return lax.ppermute(value, AXES, pairs)  28.9 us
    concatenate x11, other arithmetic, join(): return lax.optimization_barrier(jnp.concatenate(values, axis=0))  8.25 us
    unnamed x35, local copies, waits for them, and re-layouts  7.54 us
  transfers between devices with their start and end apart: 16, of which 12 were waited for; matrix products, arithmetic and copies ran while one was open for 5% of the time, Pallas kernels for 28%

profile of v1, /device:TPU:1, one launch (start us, length us, event | category | flops | bytes accessed | tf_op | source)
XLA Modules:
  0.0 152.8 jit_solution(4739156480785278298)
XLA Ops:
  0.0 0.8 convert_bitcast_fusion.1
  0.8 0.7 convert.34
  1.5 1.0 fusion.31
  2.6 2.5 %collective-permute-start.2 = (bf16[144,768]{1,0:T(8,128)(2,1)S(1)}, bf16[144,768]{1,0:T(8,128)(2,1)S(1)}, u32[]{:S(2)}, u32[]{:S(2)}) collective-permute-start(bf16[144,768]{1,0:T(8,128)(2,1)S(1)} %pad_maximum_fusion.12), channel_id=1, source_target_pairs={{0,8},{32,34},{1,9},{33,35},{64,72},{96,98},{65,73},{97,99},{2,10}... | collective-permute-start | bytes 663560 | tf_op jit(solution)/shard_map/ppermute | solution.py:34
  5.1 2.3 %collective-permute-start.6 = (bf16[144,768]{1,0:T(8,128)(2,1)S(1)}, bf16[144,768]{1,0:T(8,128)(2,1)S(1)}, u32[]{:S(2)}, u32[]{:S(2)}) collective-permute-start(bf16[144,768]{1,0:T(8,128)(2,1)S(1)} %pad_maximum_fusion.13), channel_id=1, source_target_pairs={{0,24},{32,38},{1,25},{33,39},{64,88},{96,102},{65,89},{97,103},{2... | collective-permute-start | bytes 663560 | tf_op jit(solution)/shard_map/ppermute | solution.py:34
  7.5 1.3 collective-permute-done.2
  8.8 2.6 %collective-permute-start.3 = (bf16[288,768]{1,0:T(8,128)(2,1)S(1)}, bf16[288,768]{1,0:T(8,128)(2,1)S(1)}, u32[]{:S(2)}, u32[]{:S(2)}) collective-permute-start(bf16[288,768]{1,0:T(8,128)(2,1)S(1)} %pad_maximum_fusion.9), channel_id=1, source_target_pairs={{0,2},{32,56},{1,3},{33,57},{64,66},{96,120},{65,67},{97,121},{2,0... | collective-permute-start | bytes 1327112 | tf_op jit(solution)/shard_map/ppermute | solution.py:34
  11.3 0.2 collective-permute-done.6
  11.5 1.0 collective-permute-start.7
  12.5 4.7 %collective-permute-done.3 = bf16[288,768]{1,0:T(8,128)(2,1)S(1)} collective-permute-done((bf16[288,768]{1,0:T(8,128)(2,1)S(1)}, bf16[288,768]{1,0:T(8,128)(2,1)S(1)}, u32[]{:S(2)}, u32[]{:S(2)}) %collective-permute-start.3) | collective-permute-done | bytes 442400 | tf_op jit(solution)/shard_map/ppermute | solution.py:34
  17.2 0.1 pad_maximum_fusion.6.refs_3_
  17.3 1.8 %collective-permute-done.7 = bf16[288,768]{1,0:T(8,128)(2,1)S(1)} collective-permute-done((bf16[288,768]{1,0:T(8,128)(2,1)S(1)}, bf16[288,768]{1,0:T(8,128)(2,1)S(1)}, u32[]{:S(2)}, u32[]{:S(2)}) %collective-permute-start.7) | collective-permute-done | bytes 442400 | tf_op jit(solution)/shard_map/ppermute | solution.py:34
  19.1 0.1 pad_maximum_fusion.7.refs_4_
  19.1 3.5 %collective-permute-start.4 = (bf16[576,768]{1,0:T(8,128)(2,1)S(1)}, bf16[576,768]{1,0:T(8,128)(2,1)S(1)}, u32[]{:S(2)}, u32[]{:S(2)}) collective-permute-start(bf16[576,768]{1,0:T(8,128)(2,1)S(1)} %pad_maximum_fusion.6.refs_3_), channel_id=1, source_target_pairs={{0,24},{32,38},{1,25},{33,39},{64,88},{96,102},{65,89},{97,103},{2... | collective-permute-start | bytes 2654216 | tf_op jit(solution)/shard_map/ppermute | solution.py:34
  22.6 0.0 collective-permute-start.8
  22.6 10.7 %collective-permute-done.4.refs_3_ = bf16[576,768]{1,0:T(8,128)(2,1)S(1)} collective-permute-done((bf16[576,768]{1,0:T(8,128)(2,1)S(1)}, bf16[576,768]{1,0:T(8,128)(2,1)S(1)}, u32[]{:S(2)}, u32[]{:S(2)}) %collective-permute-start.4) | collective-permute-done | bytes 884768 | tf_op jit(solution)/shard_map/ppermute | solution.py:34
  33.4 1.5 collective-permute-done.8.refs_4_
  34.8 2.2 %pad_maximum_fusion.1 = (bf16[1152,768]{1,0:T(8,128)(2,1)}, bf16[1152,768]{1,0:T(8,128)(2,1)S(1)}, bf16[1152,768]{1,0:T(8,128)(2,1)}, bf16[1152,768]{1,0:T(8,128)(2,1)S(1)}) fusion(bf16[576,768]{1,0:T(8,128)(2,1)S(1)} %pad_maximum_fusion.6.refs_3_, bf16[576,768]{1,0:T(8,128)(2,1)S(1)} %pad_maximum_fusion.7.refs_4_, ...), kind=kLoop, calls=%fused_computation.1 | loop fusion | flops 12386304 | bytes 10616832 | tf_op jit(solution)/shard_map/concatenate | solution.py:169
  37.0 0.1 collective-permute-start.5
  37.1 0.0 copy-start.16
  37.1 0.0 copy-start.15
  37.2 1.5 %collective-permute-start.9 = (bf16[1152,768]{1,0:T(8,128)(2,1)S(1)}, bf16[1152,768]{1,0:T(8,128)(2,1)S(1)}, u32[]{:S(2)}, u32[]{:S(2)}) collective-permute-start(bf16[1152,768]{1,0:T(8,128)(2,1)S(1)} %get-tuple-element.14), channel_id=1, source_target_pairs={{0,2},{32,56},{1,3},{33,57},{64,66},{96,120},{65,67},{97,121},{2,0... | collective-permute-start | bytes 5308424 | tf_op jit(solution)/shard_map/ppermute | solution.py:34
  38.7 20.1 %collective-permute-done.5.refs_3_ = bf16[1152,768]{1,0:T(8,128)(2,1)S(1)} collective-permute-done((bf16[1152,768]{1,0:T(8,128)(2,1)S(1)}, bf16[1152,768]{1,0:T(8,128)(2,1)S(1)}, u32[]{:S(2)}, u32[]{:S(2)}) %collective-permute-start.5) | collective-permute-done | bytes 1769504 | tf_op jit(solution)/shard_map/ppermute | solution.py:34
  58.8 1.3 collective-permute-done.9.refs_4_
  60.1 2.1 %pad_maximum_fusion = bf16[2304,768]{1,0:T(8,128)(2,1)} fusion(bf16[1152,768]{1,0:T(8,128)(2,1)S(1)} %collective-permute-done.9.refs_4_, bf16[1152,768]{1,0:T(8,128)(2,1)S(1)} %collective-permute-done.5.refs_3_), kind=kLoop, calls=%fused_computation | loop fusion | flops 7077888 | bytes 7077888 | tf_op jit(solution)/shard_map/concatenate | solution.py:169
  62.3 0.2 copy-done.3
  62.4 6.6 %collective-permute-start.10 = (bf16[2304,768]{1,0:T(8,128)(2,1)}, bf16[2304,768]{1,0:T(8,128)(2,1)S(1)}, u32[]{:S(2)}, u32[]{:S(2)}) collective-permute-start(bf16[2304,768]{1,0:T(8,128)(2,1)} %pad_maximum_fusion), channel_id=1, source_target_pairs={{0,32},{32,0},{1,33},{33,1},{64,96},{96,64},{65,97},{97,65},{2,34}... | collective-permute-start | bytes 10616840 | tf_op jit(solution)/shard_map/ppermute | solution.py:34
  69.1 2.8 %collective-permute-start = (bf16[272,768]{1,0:T(8,128)(2,1)S(1)}, bf16[272,768]{1,0:T(8,128)(2,1)S(1)}, u32[]{:S(2)}, u32[]{:S(2)}) collective-permute-start(bf16[272,768]{1,0:T(8,128)(2,1)S(1)} %pad_maximum_fusion.11), channel_id=1, source_target_pairs={{0,1},{32,97},{1,0},{33,96},{64,65},{96,33},{65,64},{97,32},{2,3},... | collective-permute-start | bytes 1253384 | tf_op jit(solution)/shard_map/ppermute | solution.py:34
  71.9 0.0 collective-permute-start.12
  71.9 5.4 %collective-permute-done = bf16[272,768]{1,0:T(8,128)(2,1)S(1)} collective-permute-done((bf16[272,768]{1,0:T(8,128)(2,1)S(1)}, bf16[272,768]{1,0:T(8,128)(2,1)S(1)}, u32[]{:S(2)}, u32[]{:S(2)}) %collective-permute-start) | collective-permute-done | bytes 417824 | tf_op jit(solution)/shard_map/ppermute | solution.py:34
  77.4 1.0 pad_maximum_fusion.8
  78.3 0.3 collective-permute-start.1
  78.6 2.6 %collective-permute-start.11 = (bf16[1152,768]{1,0:T(8,128)(2,1)}, bf16[1152,768]{1,0:T(8,128)(2,1)}, u32[]{:S(2)}, u32[]{:S(2)}) collective-permute-start(bf16[1152,768]{1,0:T(8,128)(2,1)} %get-tuple-element.15), channel_id=1, source_target_pairs={{0,32},{32,0},{1,33},{33,1},{64,96},{96,64},{65,97},{97,65},{2,34}... | collective-permute-start | bytes 5308424 | tf_op jit(solution)/shard_map/ppermute | solution.py:34
  81.2 1.5 %copy.8 = s32[109,109]{0,1:T(8,128)} copy(s32[109,109]{1,0:T(8,128)} %param.7) | data formatting | bytes 95048 | tf_op args[3]
  82.8 0.9 fusion.2
  83.6 0.6 pad.16.table_ref
  84.2 6.1 %collective-permute-done.1 = bf16[544,768]{1,0:T(8,128)(2,1)} collective-permute-done((bf16[544,768]{1,0:T(8,128)(2,1)}, bf16[544,768]{1,0:T(8,128)(2,1)}, u32[]{:S(2)}, u32[]{:S(2)}) %collective-permute-start.1) | collective-permute-done | bytes 835616 | tf_op jit(solution)/shard_map/ppermute | solution.py:34
  90.3 2.7 %pad_maximum_fusion.5.line_ref.refs_2_ = bf16[1088,768]{1,0:T(8,128)(2,1)} fusion(bf16[544,768]{1,0:T(8,128)(2,1)} %collective-permute-done.1, bf16[544,768]{1,0:T(8,128)(2,1)} %pad_maximum_fusion.8), kind=kLoop, calls=%fused_computation.5 | loop fusion | flops 3342336 | bytes 3342336 | tf_op jit(solution)/shard_map/concatenate | solution.py:169
  93.0 2.6 %prepare.1 = (bf16[1024,128]{1,0:T(8,128)(2,1)}, f32[1024,128]{1,0:T(8,128)}) custom-call(bf16[1088,768]{1,0:T(8,128)(2,1)} %pad_maximum_fusion.5.line_ref.refs_2_, bf16[128,128]{1,0:T(8,128)(2,1)} %pad.16.table_ref), custom_call_target="tpu_custom_call" | custom-call | flops 536870912 | tf_op jit(solution)/shard_map/prepare/pallas_call | solution.py:75
  95.6 1.4 copy-done
  97.1 1.0 copy-done.5
  98.1 0.9 copy-done.6
  99.1 1.2 copy-done.8
  100.2 1.2 copy-done.10
  101.4 5.9 %pairs.9.refs_4_ = f32[1024,768]{1,0:T(8,128)S(1)} custom-call(bf16[1024,128]{1,0:T(8,128)(2,1)S(1)} %copy-done.6, f32[1024,128]{1,0:T(8,128)S(1)} %copy-done.5, bf16[1088,768]{1,0:T(8,128)(2,1)S(1)} %copy-done, bf16[576,768]{1,0:T(8,128)(2,1)S(1)} %copy-done.8, bf16[576,768]{1,0:T(8,128)(2,1)S(1)} %copy-done.10), custom_call_target="tpu_custom_call" | custom-call | flops 3221225472 | tf_op jit(solution)/shard_map/pairs/pallas_call | solution.py:146
  107.3 0.0 collective-permute-done.12.refs_3_
  107.3 6.8 %pairs.10.refs_5_ = f32[1024,768]{1,0:T(8,128)S(1)} custom-call(bf16[1024,128]{1,0:T(8,128)(2,1)S(1)} %copy-done.6, f32[1024,128]{1,0:T(8,128)S(1)} %copy-done.5, bf16[1088,768]{1,0:T(8,128)(2,1)S(1)} %copy-done, bf16[1152,768]{1,0:T(8,128)(2,1)} %collective-permute-done.12.refs_3_, f32[1024,768]{1,0:T(8,128)S(1)} %pairs.9.refs_4_), custom_call_target="tpu_custom_call", output_to_operand_aliasing={{}: (4, {})} | custom-call | flops 3221225472 | tf_op jit(solution)/shard_map/pairs/pallas_call | solution.py:146
  114.1 5.2 %pairs.11.refs_4_ = f32[1024,768]{1,0:T(8,128)S(1)} custom-call(bf16[1024,128]{1,0:T(8,128)(2,1)S(1)} %copy-done.6, f32[1024,128]{1,0:T(8,128)S(1)} %copy-done.5, bf16[1088,768]{1,0:T(8,128)(2,1)S(1)} %copy-done, bf16[576,768]{1,0:T(8,128)(2,1)S(1)} %copy-done.12, bf16[576,768]{1,0:T(8,128)(2,1)S(1)} %copy-done.14, ...), custom_call_target="tpu_custom_call", output_to_operand_aliasing={{}: (5, {})} | custom-call | flops 3221225472 | tf_op jit(solution)/shard_map/pairs/pallas_call | solution.py:146
  119.4 6.8 %pairs.12.refs_6_.refs_5_ = f32[1024,768]{1,0:T(8,128)S(1)} custom-call(bf16[1024,128]{1,0:T(8,128)(2,1)S(1)} %copy-done.6, f32[1024,128]{1,0:T(8,128)S(1)} %copy-done.5, bf16[1088,768]{1,0:T(8,128)(2,1)S(1)} %copy-done, bf16[1152,768]{1,0:T(8,128)(2,1)} %collective-permute-done.11.refs_3_, ...), custom_call_target="tpu_custom_call", output_to_operand_aliasing={{}: (4, {})} | custom-call | flops 3221225472 | tf_op jit(solution)/shard_map/pairs/pallas_call | solution.py:146
  126.2 4.6 %pairs.15.refs_4_ = f32[512,768]{1,0:T(8,128)S(1)} custom-call(bf16[1024,128]{1,0:T(8,128)(2,1)S(1)} %copy-done.6, f32[1024,128]{1,0:T(8,128)S(1)} %copy-done.5, bf16[1088,768]{1,0:T(8,128)(2,1)S(1)} %copy-done, bf16[1152,768]{1,0:T(8,128)(2,1)S(1)} %copy-done.2, bf16[1152,768]{1,0:T(8,128)(2,1)S(1)} %copy-done.4, f32[1024,768]{1,0:T(8,128)S(1)} %pairs.12.refs_6_.refs_5_), custom_call_target="tpu_custom_call" | custom-call | flops 3221225472 | tf_op jit(solution)/shard_map/pairs/pallas_call | solution.py:146
  130.8 0.0 collective-permute-done.10.refs_5_.refs_3_
  130.8 2.3 %pairs.17 = f32[256,768]{1,0:T(8,128)S(1)} custom-call(bf16[1024,128]{1,0:T(8,128)(2,1)S(1)} %copy-done.6, f32[1024,128]{1,0:T(8,128)S(1)} %copy-done.5, bf16[1088,768]{1,0:T(8,128)(2,1)S(1)} %copy-done, bf16[2304,768]{1,0:T(8,128)(2,1)S(1)} %collective-permute-done.10.refs_5_.refs_3_, f32[512,768]{1,0:T(8,128)S(1)} %pairs.15.refs_4_), custom_call_target="tpu_custom_call" | custom-call | flops 1610612736 | tf_op jit(solution)/shard_map/pairs/pallas_call | solution.py:146
  133.1 0.1 multiply_convert_fusion.1
  133.2 3.0 %collective-permute-start.14 = (f16[256,768]{1,0:T(8,128)(2,1)S(1)}, f16[256,768]{1,0:T(8,128)(2,1)S(1)}, u32[]{:S(2)}, u32[]{:S(2)}) collective-permute-start(f16[256,768]{1,0:T(8,128)(2,1)S(1)} %multiply_convert_fusion.1), channel_id=1, source_target_pairs={{0,1},{32,97},{1,0},{33,96},{64,65},{96,33},{65,64},{97,32},{2,3},... | collective-permute-start | bytes 1179656 | tf_op jit(solution)/shard_map/ppermute | solution.py:34
  136.2 4.2 %pairs.14 = f32[256,768]{1,0:T(8,128)S(1)} custom-call(bf16[1024,128]{1,0:T(8,128)(2,1)S(1)} %copy-done.6, f32[1024,128]{1,0:T(8,128)S(1)} %copy-done.5, bf16[1088,768]{1,0:T(8,128)(2,1)S(1)} %copy-done, bf16[1152,768]{1,0:T(8,128)(2,1)S(1)} %copy-done.2, bf16[1152,768]{1,0:T(8,128)(2,1)S(1)} %copy-done.4, ...), custom_call_target="tpu_custom_call" | custom-call | flops 3221225472 | tf_op jit(solution)/shard_map/pairs/pallas_call | solution.py:146
  140.4 0.1 multiply_convert_fusion.2
  140.5 0.1 collective-permute-start.13
  140.6 2.3 %pairs.16 = f32[256,768]{1,0:T(8,128)S(1)} custom-call(bf16[1024,128]{1,0:T(8,128)(2,1)S(1)} %copy-done.6, f32[1024,128]{1,0:T(8,128)S(1)} %copy-done.5, bf16[1088,768]{1,0:T(8,128)(2,1)S(1)} %copy-done, bf16[2304,768]{1,0:T(8,128)(2,1)S(1)} %collective-permute-done.10.refs_5_.refs_3_, f32[512,768]{1,0:T(8,128)S(1)} %pairs.15.refs_4_), custom_call_target="tpu_custom_call" | custom-call | flops 1610612736 | tf_op jit(solution)/shard_map/pairs/pallas_call | solution.py:146
  142.8 0.1 multiply_convert_fusion
  143.0 0.1 collective-permute-start.15
  143.1 4.2 %pairs.13 = f32[256,768]{1,0:T(8,128)S(1)} custom-call(bf16[1024,128]{1,0:T(8,128)(2,1)S(1)} %copy-done.6, f32[1024,128]{1,0:T(8,128)S(1)} %copy-done.5, bf16[1088,768]{1,0:T(8,128)(2,1)S(1)} %copy-done, bf16[1152,768]{1,0:T(8,128)(2,1)S(1)} %copy-done.2, bf16[1152,768]{1,0:T(8,128)(2,1)S(1)} %copy-done.4, ...), custom_call_target="tpu_custom_call" | custom-call | flops 3221225472 | tf_op jit(solution)/shard_map/pairs/pallas_call | solution.py:146
  147.3 1.1 collective-permute-done.13
  148.4 3.4 %collective-permute-done.15 = f16[256,768]{1,0:T(8,128)(2,1)S(1)} collective-permute-done((f16[256,768]{1,0:T(8,128)(2,1)S(1)}, f16[256,768]{1,0:T(8,128)(2,1)S(1)}, u32[]{:S(2)}, u32[]{:S(2)}) %collective-permute-start.15) | collective-permute-done | bytes 393248 | tf_op jit(solution)/shard_map/ppermute | solution.py:34
  151.8 1.0 multiply_add_fusion
  (42 shorter events, 0.3 us)
Async XLA Ops:
  2.6 6.2 %collective-permute-start.2 = (bf16[144,768]{1,0:T(8,128)(2,1)S(1)}, bf16[144,768]{1,0:T(8,128)(2,1)S(1)}, u32[]{:S(2)}, u32[]{:S(2)}) collective-permute-start(bf16[144,768]{1,0:T(8,128)(2,1)S(1)} %pad_maximum_fusion.12), channel_id=1, source_target_pairs={{0,8},{32,34},{1,9},{33,35},{64,72},{96,98},{65,73},{97,99},{2,10}... | collective-permute-start | bytes 663560 | tf_op jit(solution)/shard_map/ppermute | solution.py:34
  5.1 6.4 %collective-permute-start.6 = (bf16[144,768]{1,0:T(8,128)(2,1)S(1)}, bf16[144,768]{1,0:T(8,128)(2,1)S(1)}, u32[]{:S(2)}, u32[]{:S(2)}) collective-permute-start(bf16[144,768]{1,0:T(8,128)(2,1)S(1)} %pad_maximum_fusion.13), channel_id=1, source_target_pairs={{0,24},{32,38},{1,25},{33,39},{64,88},{96,102},{65,89},{97,103},{2... | collective-permute-start | bytes 663560 | tf_op jit(solution)/shard_map/ppermute | solution.py:34
  8.8 8.4 %collective-permute-start.3 = (bf16[288,768]{1,0:T(8,128)(2,1)S(1)}, bf16[288,768]{1,0:T(8,128)(2,1)S(1)}, u32[]{:S(2)}, u32[]{:S(2)}) collective-permute-start(bf16[288,768]{1,0:T(8,128)(2,1)S(1)} %pad_maximum_fusion.9), channel_id=1, source_target_pairs={{0,2},{32,56},{1,3},{33,57},{64,66},{96,120},{65,67},{97,121},{2,0... | collective-permute-start | bytes 1327112 | tf_op jit(solution)/shard_map/ppermute | solution.py:34
  11.5 7.5 %collective-permute-start.7 = (bf16[288,768]{1,0:T(8,128)(2,1)S(1)}, bf16[288,768]{1,0:T(8,128)(2,1)S(1)}, u32[]{:S(2)}, u32[]{:S(2)}) collective-permute-start(bf16[288,768]{1,0:T(8,128)(2,1)S(1)} %pad_maximum_fusion.10), channel_id=1, source_target_pairs={{0,6},{32,40},{1,7},{33,41},{64,70},{96,104},{65,71},{97,105},{2,4... | collective-permute-start | bytes 1327112 | tf_op jit(solution)/shard_map/ppermute | solution.py:34
  17.3 19.7 %copy-start.7 = (bf16[576,768]{1,0:T(8,128)(2,1)}, bf16[576,768]{1,0:T(8,128)(2,1)S(1)}, u32[]{:S(2)}) copy-start(bf16[576,768]{1,0:T(8,128)(2,1)S(1)} %pad_maximum_fusion.6.refs_3_) | copy-start | bytes 2654212
  19.1 17.9 %copy-start.9 = (bf16[576,768]{1,0:T(8,128)(2,1)}, bf16[576,768]{1,0:T(8,128)(2,1)S(1)}, u32[]{:S(2)}) copy-start(bf16[576,768]{1,0:T(8,128)(2,1)S(1)} %pad_maximum_fusion.7.refs_4_) | copy-start | bytes 2654212
  19.1 14.2 %collective-permute-start.4 = (bf16[576,768]{1,0:T(8,128)(2,1)S(1)}, bf16[576,768]{1,0:T(8,128)(2,1)S(1)}, u32[]{:S(2)}, u32[]{:S(2)}) collective-permute-start(bf16[576,768]{1,0:T(8,128)(2,1)S(1)} %pad_maximum_fusion.6.refs_3_), channel_id=1, source_target_pairs={{0,24},{32,38},{1,25},{33,39},{64,88},{96,102},{65,89},{97,103},{2... | collective-permute-start | bytes 2654216 | tf_op jit(solution)/shard_map/ppermute | solution.py:34
  22.6 12.2 %collective-permute-start.8 = (bf16[576,768]{1,0:T(8,128)(2,1)S(1)}, bf16[576,768]{1,0:T(8,128)(2,1)S(1)}, u32[]{:S(2)}, u32[]{:S(2)}) collective-permute-start(bf16[576,768]{1,0:T(8,128)(2,1)S(1)} %pad_maximum_fusion.7.refs_4_), channel_id=1, source_target_pairs={{0,8},{32,34},{1,9},{33,35},{64,72},{96,98},{65,73},{97,99},{2,10}... | collective-permute-start | bytes 2654216 | tf_op jit(solution)/shard_map/ppermute | solution.py:34
  33.4 3.7 %copy-start.11 = (bf16[576,768]{1,0:T(8,128)(2,1)}, bf16[576,768]{1,0:T(8,128)(2,1)S(1)}, u32[]{:S(2)}) copy-start(bf16[576,768]{1,0:T(8,128)(2,1)S(1)} %collective-permute-done.4.refs_3_) | copy-start | bytes 2654212
  34.8 2.2 %copy-start.13 = (bf16[576,768]{1,0:T(8,128)(2,1)}, bf16[576,768]{1,0:T(8,128)(2,1)S(1)}, u32[]{:S(2)}) copy-start(bf16[576,768]{1,0:T(8,128)(2,1)S(1)} %collective-permute-done.8.refs_4_) | copy-start | bytes 2654212
  37.0 21.7 %collective-permute-start.5 = (bf16[1152,768]{1,0:T(8,128)(2,1)S(1)}, bf16[1152,768]{1,0:T(8,128)(2,1)S(1)}, u32[]{:S(2)}, u32[]{:S(2)}) collective-permute-start(bf16[1152,768]{1,0:T(8,128)(2,1)S(1)} %get-tuple-element.16), channel_id=1, source_target_pairs={{0,6},{32,40},{1,7},{33,41},{64,70},{96,104},{65,71},{97,105},{2,4... | collective-permute-start | bytes 5308424 | tf_op jit(solution)/shard_map/ppermute | solution.py:34
  37.1 31.9 %copy-start.16 = (s32[256]{0:T(256)S(1)}, s32[256]{0:T(256)}, u32[]{:S(2)}) copy-start(s32[256]{0:T(256)} %param.6) | copy-start | bytes 3076
  37.1 31.9 %copy-start.15 = (bf16[256,768]{1,0:T(8,128)(2,1)S(1)}, bf16[256,768]{1,0:T(8,128)(2,1)}, u32[]{:S(2)}) copy-start(bf16[256,768]{1,0:T(8,128)(2,1)} %param.4) | copy-start | bytes 1179652
  37.2 23.0 %collective-permute-start.9 = (bf16[1152,768]{1,0:T(8,128)(2,1)S(1)}, bf16[1152,768]{1,0:T(8,128)(2,1)S(1)}, u32[]{:S(2)}, u32[]{:S(2)}) collective-permute-start(bf16[1152,768]{1,0:T(8,128)(2,1)S(1)} %get-tuple-element.14), channel_id=1, source_target_pairs={{0,2},{32,56},{1,3},{33,57},{64,66},{96,120},{65,67},{97,121},{2,0... | collective-permute-start | bytes 5308424 | tf_op jit(solution)/shard_map/ppermute | solution.py:34
  58.8 3.5 %copy-start.1 = (bf16[1152,768]{1,0:T(8,128)(2,1)}, bf16[1152,768]{1,0:T(8,128)(2,1)S(1)}, u32[]{:S(2)}) copy-start(bf16[1152,768]{1,0:T(8,128)(2,1)S(1)} %collective-permute-done.5.refs_3_) | copy-start | bytes 5308420
  60.1 2.3 %copy-start.3 = (bf16[1152,768]{1,0:T(8,128)(2,1)}, bf16[1152,768]{1,0:T(8,128)(2,1)S(1)}, u32[]{:S(2)}) copy-start(bf16[1152,768]{1,0:T(8,128)(2,1)S(1)} %collective-permute-done.9.refs_4_) | copy-start | bytes 5308420
  62.4 68.4 %collective-permute-start.10 = (bf16[2304,768]{1,0:T(8,128)(2,1)}, bf16[2304,768]{1,0:T(8,128)(2,1)S(1)}, u32[]{:S(2)}, u32[]{:S(2)}) collective-permute-start(bf16[2304,768]{1,0:T(8,128)(2,1)} %pad_maximum_fusion), channel_id=1, source_target_pairs={{0,32},{32,0},{1,33},{33,1},{64,96},{96,64},{65,97},{97,65},{2,34}... | collective-permute-start | bytes 10616840 | tf_op jit(solution)/shard_map/ppermute | solution.py:34
  69.1 8.2 %collective-permute-start = (bf16[272,768]{1,0:T(8,128)(2,1)S(1)}, bf16[272,768]{1,0:T(8,128)(2,1)S(1)}, u32[]{:S(2)}, u32[]{:S(2)}) collective-permute-start(bf16[272,768]{1,0:T(8,128)(2,1)S(1)} %pad_maximum_fusion.11), channel_id=1, source_target_pairs={{0,1},{32,97},{1,0},{33,96},{64,65},{96,33},{65,64},{97,32},{2,3},... | collective-permute-start | bytes 1253384 | tf_op jit(solution)/shard_map/ppermute | solution.py:34
  71.9 35.4 %collective-permute-start.12 = (bf16[1152,768]{1,0:T(8,128)(2,1)}, bf16[1152,768]{1,0:T(8,128)(2,1)}, u32[]{:S(2)}, u32[]{:S(2)}) collective-permute-start(bf16[1152,768]{1,0:T(8,128)(2,1)} %get-tuple-element.13), channel_id=1, source_target_pairs={{0,32},{32,0},{1,33},{33,1},{64,96},{96,64},{65,97},{97,65},{2,34}... | collective-permute-start | bytes 5308424 | tf_op jit(solution)/shard_map/ppermute | solution.py:34
  78.3 12.0 %collective-permute-start.1 = (bf16[544,768]{1,0:T(8,128)(2,1)}, bf16[544,768]{1,0:T(8,128)(2,1)}, u32[]{:S(2)}, u32[]{:S(2)}) collective-permute-start(bf16[544,768]{1,0:T(8,128)(2,1)} %pad_maximum_fusion.8), channel_id=1, source_target_pairs={{0,65},{32,33},{1,64},{33,32},{64,1},{96,97},{65,0},{97,96},{2,67}... | collective-permute-start | bytes 2506760 | tf_op jit(solution)/shard_map/ppermute | solution.py:34
  78.6 40.7 %collective-permute-start.11 = (bf16[1152,768]{1,0:T(8,128)(2,1)}, bf16[1152,768]{1,0:T(8,128)(2,1)}, u32[]{:S(2)}, u32[]{:S(2)}) collective-permute-start(bf16[1152,768]{1,0:T(8,128)(2,1)} %get-tuple-element.15), channel_id=1, source_target_pairs={{0,32},{32,0},{1,33},{33,1},{64,96},{96,64},{65,97},{97,65},{2,34}... | collective-permute-start | bytes 5308424 | tf_op jit(solution)/shard_map/ppermute | solution.py:34
  95.6 1.4 copy-start
  97.1 1.0 copy-start.5
  98.1 0.9 copy-start.6
  99.1 1.2 copy-start.8
  100.2 1.2 copy-start.10
  107.3 6.9 %copy-start.12 = (bf16[576,768]{1,0:T(8,128)(2,1)S(1)}, bf16[576,768]{1,0:T(8,128)(2,1)}, u32[]{:S(2)}) copy-start(bf16[576,768]{1,0:T(8,128)(2,1)} %copy-done.11) | copy-start | bytes 2654212
  107.3 6.9 %copy-start.14 = (bf16[576,768]{1,0:T(8,128)(2,1)S(1)}, bf16[576,768]{1,0:T(8,128)(2,1)}, u32[]{:S(2)}) copy-start(bf16[576,768]{1,0:T(8,128)(2,1)} %copy-done.13) | copy-start | bytes 2654212
  119.4 6.9 %copy-start.2 = (bf16[1152,768]{1,0:T(8,128)(2,1)S(1)}, bf16[1152,768]{1,0:T(8,128)(2,1)}, u32[]{:S(2)}) copy-start(bf16[1152,768]{1,0:T(8,128)(2,1)} %copy-done.1) | copy-start | bytes 5308420
  119.4 6.9 %copy-start.4 = (bf16[1152,768]{1,0:T(8,128)(2,1)S(1)}, bf16[1152,768]{1,0:T(8,128)(2,1)}, u32[]{:S(2)}) copy-start(bf16[1152,768]{1,0:T(8,128)(2,1)} %copy-done.3) | copy-start | bytes 5308420
  133.2 9.7 %collective-permute-start.14 = (f16[256,768]{1,0:T(8,128)(2,1)S(1)}, f16[256,768]{1,0:T(8,128)(2,1)S(1)}, u32[]{:S(2)}, u32[]{:S(2)}) collective-permute-start(f16[256,768]{1,0:T(8,128)(2,1)S(1)} %multiply_convert_fusion.1), channel_id=1, source_target_pairs={{0,1},{32,97},{1,0},{33,96},{64,65},{96,33},{65,64},{97,32},{2,3},... | collective-permute-start | bytes 1179656 | tf_op jit(solution)/shard_map/ppermute | solution.py:34
  140.5 7.9 %collective-permute-start.13 = (f16[256,768]{1,0:T(8,128)(2,1)S(1)}, f16[256,768]{1,0:T(8,128)(2,1)S(1)}, u32[]{:S(2)}, u32[]{:S(2)}) collective-permute-start(f16[256,768]{1,0:T(8,128)(2,1)S(1)} %multiply_convert_fusion.2), channel_id=1, source_target_pairs={{0,1},{32,97},{1,0},{33,96},{64,65},{96,33},{65,64},{97,32},{2,3},... | collective-permute-start | bytes 1179656 | tf_op jit(solution)/shard_map/ppermute | solution.py:34
  143.0 8.8 %collective-permute-start.15 = (f16[256,768]{1,0:T(8,128)(2,1)S(1)}, f16[256,768]{1,0:T(8,128)(2,1)S(1)}, u32[]{:S(2)}, u32[]{:S(2)}) collective-permute-start(f16[256,768]{1,0:T(8,128)(2,1)S(1)} %multiply_convert_fusion), channel_id=1, source_target_pairs={{0,65},{32,33},{1,64},{33,32},{64,1},{96,97},{65,0},{97,96},{2,67}... | collective-permute-start | bytes 1179656 | tf_op jit(solution)/shard_map/ppermute | solution.py:34

commit v2 on v1

v2 whole, which is shorter than its diff:
```python
import functools
import math

import jax
import jax.numpy as jnp
from jax import lax
from jax.experimental import pallas as pl
from jax.experimental.pallas import tpu as pltpu
from jax.sharding import PartitionSpec as P


AXES = ("grp", "dev")
NT = (((1,), (1,)), ((), ()))
NN = (((1,), (0,)), ((), ()))
TN = (((0,), (0,)), ((), ()))
LANES = 128
LINK_SCALE = 16.0
BLOCK = 256
META = 16


def position(x, z, y, core):
    return ((y >> 1) * 2 + core) * 32 + x * 8 + z * 2 + (y & 1)


def exchange(value, step):
    pairs = []
    for x in range(4):
        for z in range(4):
            for y in range(4):
                for core in range(2):
                    dx, dz, dy, dc = step(core)
                    pairs.append((position(x, z, y, core), position(x ^ dx, z ^ dz, y ^ dy, core ^ dc)))
    return lax.ppermute(value, AXES, pairs)


PLANE = ((1, 0, 0, 0), (0, 1, 0, 0), (3, 0, 0, 0), (0, 3, 0, 0))
LINE = ((0, 0, 1, 0), (0, 0, 3, 0))


def plane_step(stream, k):
    return lambda core: PLANE[(k + 2 * stream + core) % 4]


def line_step(k):
    return lambda core: LINE[(k + core) % 2]


def partner(core):
    return (0, 0, 0, 1)


def in_vmem(count):
    return [pl.BlockSpec(memory_space=pltpu.VMEM)] * count


def pack_body(rows_ref, language_ref, group_ref, mask_ref, line_ref, first_ref, second_ref, table_ref, square_ref):
    width = rows_ref.shape[1]
    language = language_ref[...].astype(jnp.float32)
    group = group_ref[...]
    digits = [language, (group // LANES).astype(jnp.float32), (group % LANES).astype(jnp.float32)]

    def row_of(values):
        row = jnp.concatenate(values, axis=1)
        if row.shape[1] < width:
            row = jnp.concatenate([row, jnp.zeros((1, width - row.shape[1]), jnp.float32)], axis=1)
        return jnp.broadcast_to(row, (META, width)).astype(jnp.bfloat16)

    count = mask_ref.shape[0]
    square_ref[...] = jnp.zeros_like(square_ref)
    square_ref[:count, :count] = mask_ref[...].astype(jnp.float32)
    square = square_ref[...]
    table_ref[...] = ((square + square.T) * 0.5).astype(jnp.bfloat16)
    line_ref[:BLOCK, :] = rows_ref[...]
    line_ref[BLOCK:, :] = row_of([d[h:h + 1] for d in digits for h in range(2)])
    for h, ref in enumerate((first_ref, second_ref)):
        ref[:LANES, :] = rows_ref[h * LANES:(h + 1) * LANES, :]
        ref[LANES:, :] = row_of([d[h:h + 1] for d in digits])


def pack(embeddings, language, sentence_group, pair_mask):
    width = embeddings.shape[1]
    shapes = [(BLOCK + META, width), (LANES + META, width), (LANES + META, width), (LANES, LANES)]
    return pl.pallas_call(
        pack_body,
        in_specs=in_vmem(4),
        out_specs=in_vmem(4),
        out_shape=[pltpu.VMEM(shape, jnp.bfloat16) for shape in shapes],
        scratch_shapes=[pltpu.VMEM((LANES, LANES), jnp.float32)],
        name="pack",
    )(embeddings, language.reshape(2, LANES), sentence_group.reshape(2, LANES), pair_mask)


def block_of(line_refs, b):
    return line_refs[b].at[:] if len(line_refs) == 2 else line_refs[0].at[b * (BLOCK + META):(b + 1) * (BLOCK + META)]


def lookup_rows(line_refs, table_ref):
    lang_ids = lax.broadcasted_iota(jnp.int32, (LANES, BLOCK), 0).astype(jnp.float32)
    weights, groups = [], []
    for b in range(2):
        row = block_of(line_refs, b)[BLOCK:, :].astype(jnp.float32)[:1]
        onehot = jnp.where(lang_ids == row[:, :BLOCK], 1.0, 0.0).astype(jnp.bfloat16)
        weights.append(lax.dot_general(onehot, table_ref[...], TN, preferred_element_type=jnp.float32))
        group = row[:, BLOCK:2 * BLOCK] * 128.0 + row[:, 2 * BLOCK:3 * BLOCK]
        groups.append(jnp.broadcast_to(group, (LANES, BLOCK)).T)
    return jnp.concatenate(weights, axis=0), jnp.concatenate(groups, axis=0)


def pair_body(units, line_count, first, blocks, tile, scale, diagonal, looked_up, carry_first, *refs):
    if looked_up:
        weight_ref, group_ref, *rest = refs
        out_ref = refs[-1]
    else:
        table_ref, *rest = refs
        out_ref, weight_ref, group_ref = refs[-3:]
        weight_ref[...], group_ref[...] = lookup_rows(rest[:line_count], table_ref)
    line_refs, columns = rest[:line_count], rest[line_count:line_count + len(units)]
    carry_ref = refs[-2] if carry_first is not None else None
    log_scale = scale * math.log2(math.e)
    pitch = LANES + META
    height = blocks * BLOCK
    rows = jnp.concatenate([block_of(line_refs, b)[:BLOCK, :] for b in range(first, first + blocks)], axis=0)
    table_rows = weight_ref[first * BLOCK:first * BLOCK + height, :]
    groups = group_ref[first * BLOCK:first * BLOCK + height, :]
    total = None
    if carry_ref is not None:
        total = carry_ref[carry_first * BLOCK:carry_first * BLOCK + height, :]
    share = tile // len(columns)

    def add_tile(t, total):
        pieces = []
        for side, ref in enumerate(columns):
            for p in range(share):
                at = (t * share + p) * pitch
                pieces.append((side, ref, at if isinstance(at, int) else pl.multiple_of(at, META)))
        data = jnp.concatenate([ref[pl.ds(at, LANES), :] for _, ref, at in pieces], axis=0)
        scores = lax.dot_general(rows, data, NT, preferred_element_type=jnp.float32)
        coefs = []
        for n, (side, ref, at) in enumerate(pieces):
            meta = ref[pl.ds(at + LANES, META), :].astype(jnp.float32)[:1]
            same = groups == meta[:, LANES:2 * LANES] * 128.0 + meta[:, 2 * LANES:3 * LANES]
            power = jnp.exp2(scores[:, n * LANES:(n + 1) * LANES] * jnp.where(same, log_scale, -log_scale))
            index = jnp.broadcast_to(meta[:, :LANES].astype(jnp.int32), (height, LANES))
            weights = jnp.take_along_axis(table_rows, index, axis=1)
            coef = (weights * jnp.where(same, -scale, scale)) * (1.0 / (1.0 + power))
            if diagonal and n % share == 0:
                assert share == units[0]
                row = lax.broadcasted_iota(jnp.int32, (height, LANES), 0)
                column = lax.broadcasted_iota(jnp.int32, (height, LANES), 1) + side * LANES
                coef = jnp.where(row == column, 0.0, coef)
            coefs.append(coef.astype(jnp.bfloat16))
        part = lax.dot_general(jnp.concatenate(coefs, axis=1), data, NN, preferred_element_type=jnp.float32)
        return part if total is None else total + part

    tiles = units[0] // share
    if tiles == 1 or blocks == 1:
        for t in range(tiles):
            total = add_tile(t, total)
        out_ref[...] = total
        return
    out_ref[...] = jnp.zeros((height, rows.shape[1]), jnp.float32) if total is None else total

    def one_tile(t, _):
        out_ref[...] = add_tile(t, out_ref[...])
        return 0

    lax.fori_loop(0, tiles, one_tile, 0)


def pairs(lookup, line, columns, carry, scale, first=0, blocks=2, carry_first=0, diagonal=False, tile=8):
    width = line[0].shape[1]
    looked_up = isinstance(lookup, tuple)
    units = [c.shape[0] // (LANES + META) for c in columns]
    operands = [*lookup, *line, *columns] if looked_up else [lookup, *line, *columns]
    rows, total = BLOCK * blocks, LANES * sum(units)
    aliases = {}
    if carry is not None:
        operands.append(carry)
        aliases = {len(operands) - 1: 0} if carry.shape[0] == rows else {}
    outs = [pltpu.VMEM((rows, width), jnp.float32)]
    if not looked_up:
        outs += [pltpu.VMEM((rows, LANES), jnp.float32)] * 2
    operands = [pltpu.with_memory_space_constraint(value, pltpu.VMEM) for value in operands]
    out = pl.pallas_call(
        functools.partial(
            pair_body, units, len(line), first, blocks, tile, scale, diagonal, looked_up, carry_first if carry is not None else None
        ),
        in_specs=in_vmem(len(operands)),
        out_specs=in_vmem(len(outs)),
        out_shape=outs,
        input_output_aliases=aliases,
        compiler_params=pltpu.CompilerParams(vmem_limit_bytes=8 << 20),
        cost_estimate=pl.CostEstimate(
            flops=4 * rows * total * width, transcendentals=2 * rows * total, bytes_accessed=0
        ),
        name="pairs",
    )(*operands)
    return out[0] if looked_up else out


def to_link(value):
    return (value * LINK_SCALE).astype(jnp.float16)


def from_link(value):
    return value.astype(jnp.float32) * (1.0 / LINK_SCALE)


def join(*values):
    return lax.optimization_barrier(jnp.concatenate(values, axis=0))


def gradient(embeddings, language, sentence_group, pair_mask):
    width = embeddings.shape[1]
    scale = 1.0 / math.sqrt(width)
    line, *streams, table = pack(embeddings, language, sentence_group, pair_mask)
    arrived = []
    for k in range(2):
        got = [exchange(streams[s], plane_step(s, k)) for s in range(2)]
        if k == 0:
            near = [line, exchange(line, line_step(0))]
            far = [exchange(join(*near), line_step(1))]
        for s in range(2):
            streams[s] = join(streams[s], got[s])
    arrived.append(streams)
    arrived.append([exchange(streams[s], plane_step(s, 2)) for s in range(2)])
    for n in range(2):
        arrived.append([exchange(arrived[n][s], plane_step(s, 3)) for s in range(2)])
    others = [[exchange(part[s], partner) for s in range(2)] for part in arrived]

    def step(*rest, **options):
        return pairs(*rest, scale=scale, **options)

    near_sum, *near_lookup = step(table, near, arrived[0], None, diagonal=True)
    near_lookup = tuple(near_lookup)
    near_sum = step(near_lookup, near, others[0], near_sum)
    both = [own + other for own, other in zip(arrived, others)]
    near_sum = step(near_lookup, near, both[1], near_sum)
    far_sum, *far_lookup = step(table, far, both[0], None)
    far_lookup = tuple(far_lookup)
    far_sum = step(far_lookup, far, both[1], far_sum)
    far_sum = step(far_lookup, far, both[2], far_sum)
    far_sum = step(far_lookup, far, arrived[3], far_sum)
    last = step(far_lookup, far, others[3], far_sum, first=1, blocks=1, carry_first=1)
    relay = exchange(to_link(last), line_step(0))
    near0 = step(near_lookup, near, both[2] + both[3], near_sum, first=1, blocks=1, carry_first=1)
    back0 = exchange(to_link(near0), line_step(0))
    near1 = step(far_lookup, far, others[3], far_sum, first=0, blocks=1, carry_first=0)
    back1 = exchange(to_link(near1 + from_link(relay)), line_step(1))
    final = step(near_lookup, near, both[2] + both[3], near_sum, first=0, blocks=1, carry_first=0)
    return final + from_link(back0) + from_link(back1)


def solution(mesh):
    return jax.shard_map(
        gradient,
        mesh=mesh,
        in_specs=(P(AXES, None), P(AXES), P(AXES), P()),
        out_specs=P(AXES, None),
        check_vma=False,
    )
```

time: 153 us -> 109 us (0.71)
  waiting for transfers between devices: 57.5 us -> 32.6 us
  other arithmetic: 11.9 us -> 1.59 us
  local copies, waits for them, and re-layouts: 9.22 us -> 0 us
  starting transfers between devices: 28.9 us -> 37.7 us
  Pallas kernels: 44.9 us -> 36.7 us
    ppermute x16 -> x23, waiting for transfers between devices: 57.5 us -> 32.6 us  [exchange(): return lax.ppermute(value, AXES, pairs)]
    ppermute x16 -> x23, starting transfers between devices: 28.9 us -> 37.7 us  [exchange(): return lax.ppermute(value, AXES, pairs)]
    pallas_call x10 -> x12, Pallas kernels: 44.9 us -> 36.7 us  [the longest x11 35.6 us: pairs(): pl.pallas_call(functools.partial(pair_body, units, len(line), first, bloc...]
    concatenate x11 -> x5, other arithmetic: 8.25 us -> 0.23 us  [join(): return lax.optimization_barrier(jnp.concatenate(values, axis=0))]
    unnamed x35 -> x0, local copies, waits for them, and re-layouts: 7.54 us -> none
  transfers between devices with their start and end apart: 16 -> 23, of which waited for: 12 -> 7; matrix products, arithmetic and copies ran while one was open for 5% -> 0% of each run, Pallas kernels for 28% -> 32%
where the time goes in v2:
time: 109 us
  starting transfers between devices  37.7 us (35%)
  Pallas kernels  36.7 us (34%)
  waiting for transfers between devices  32.6 us (30%)
  other arithmetic  1.59 us (1%)
    ppermute x23, starting transfers between devices, exchange(): return lax.ppermute(value, AXES, pairs)  37.7 us
    pallas_call x11, Pallas kernels, pairs(): pl.pallas_call(functools.partial(pair_body, units, len(line), first, bloc...  35.6 us
    ppermute x23, waiting for transfers between devices, exchange(): return lax.ppermute(value, AXES, pairs)  32.6 us
  transfers between devices with their start and end apart: 23, of which 7 were waited for; matrix products, arithmetic and copies ran while one was open for 0% of the time, Pallas kernels for 32%

profile of v2, /device:TPU:1, one launch (start us, length us, event | category | flops | bytes accessed | tf_op | source)
XLA Modules:
  0.0 108.8 jit_solution(7498591325152199779)
XLA Ops:
  0.0 1.2 %pack.1 = (bf16[272,768]{1,0:T(8,128)(2,1)S(1)}, bf16[144,768]{1,0:T(8,128)(2,1)S(1)}, bf16[144,768]{1,0:T(8,128)(2,1)S(1)}, bf16[128,128]{1,0:T(8,128)(2,1)S(1)}) custom-call(bf16[256,768]{1,0:T(8,128)(2,1)} %rows_ref.1, s32[2,128]{1,0:T(2,128)} %bitcast.2, s32[2,128]{1,0:T(2,128)} %bitcast.3, s32[109,109]{1,0:T(8,128)} %mask_ref.1), custom_call_target="tpu_custom_call" | custom-call | tf_op jit(solution)/shard_map/pack/pallas_call | solution.py:84
  1.2 4.7 %collective-permute-start.3 = (bf16[144,768]{1,0:T(8,128)(2,1)S(1)}, bf16[144,768]{1,0:T(8,128)(2,1)S(1)}, u32[]{:S(2)}, u32[]{:S(2)}) collective-permute-start(bf16[144,768]{1,0:T(8,128)(2,1)S(1)} %get-tuple-element.18), channel_id=1, source_target_pairs={{0,24},{32,38},{1,25},{33,39},{64,88},{96,102},{65,89},{97,103},{2... | collective-permute-start | bytes 663560 | tf_op jit(solution)/shard_map/ppermute | solution.py:34
  5.8 2.7 %collective-permute-start = (bf16[272,768]{1,0:T(8,128)(2,1)S(1)}, bf16[272,768]{1,0:T(8,128)(2,1)S(1)}, u32[]{:S(2)}, u32[]{:S(2)}) collective-permute-start(bf16[272,768]{1,0:T(8,128)(2,1)S(1)} %get-tuple-element.16.refs_1_.refs_2_), channel_id=1, source_target_pairs={{0,1},{32,97},{1,0},{33,96},{64,65},{96,33},{65,64},{97,32},{2,3},... | collective-permute-start | bytes 1253384 | tf_op jit(solution)/shard_map/ppermute | solution.py:34
  8.6 0.8 collective-permute-done.3
  9.4 1.1 collective-permute-start.4
  10.5 0.0 collective-permute-start.1
  10.5 3.5 %collective-permute-done.refs_2_.refs_3_ = bf16[272,768]{1,0:T(8,128)(2,1)S(1)} collective-permute-done((bf16[272,768]{1,0:T(8,128)(2,1)S(1)}, bf16[272,768]{1,0:T(8,128)(2,1)S(1)}, u32[]{:S(2)}, u32[]{:S(2)}) %collective-permute-start) | collective-permute-done | bytes 417824 | tf_op jit(solution)/shard_map/ppermute | solution.py:34
  14.0 0.1 pad_maximum_fusion.2
  14.1 0.4 collective-permute-start.20
  14.5 2.5 %collective-permute-done.4 = bf16[288,768]{1,0:T(8,128)(2,1)S(1)} collective-permute-done((bf16[288,768]{1,0:T(8,128)(2,1)S(1)}, bf16[288,768]{1,0:T(8,128)(2,1)S(1)}, u32[]{:S(2)}, u32[]{:S(2)}) %collective-permute-start.4) | collective-permute-done | bytes 442400 | tf_op jit(solution)/shard_map/ppermute | solution.py:34
  17.0 0.1 pad_maximum_fusion.1.refs_4_.refs_3_
  17.0 3.5 %collective-permute-start.18 = (bf16[576,768]{1,0:T(8,128)(2,1)S(1)}, bf16[576,768]{1,0:T(8,128)(2,1)S(1)}, u32[]{:S(2)}, u32[]{:S(2)}) collective-permute-start(bf16[576,768]{1,0:T(8,128)(2,1)S(1)} %pad_maximum_fusion.1.refs_4_.refs_3_), channel_id=1, source_target_pairs={{0,32},{32,0},{1,33},{33,1},{64,96},{96,64},{65,97},{97,65},{2,34}... | collective-permute-start | bytes 2654216 | tf_op jit(solution)/shard_map/ppermute | solution.py:34
  20.5 0.0 collective-permute-start.11
  20.5 0.0 collective-permute-done.1
  20.5 2.6 %collective-permute-start.2 = (bf16[288,768]{1,0:T(8,128)(2,1)S(1)}, bf16[288,768]{1,0:T(8,128)(2,1)S(1)}, u32[]{:S(2)}, u32[]{:S(2)}) collective-permute-start(bf16[288,768]{1,0:T(8,128)(2,1)S(1)} %pad_maximum_fusion.3), channel_id=1, source_target_pairs={{0,2},{32,56},{1,3},{33,57},{64,66},{96,120},{65,67},{97,121},{2,0... | collective-permute-start | bytes 1327112 | tf_op jit(solution)/shard_map/ppermute | solution.py:34
  23.1 5.9 %collective-permute-done.2 = bf16[288,768]{1,0:T(8,128)(2,1)S(1)} collective-permute-done((bf16[288,768]{1,0:T(8,128)(2,1)S(1)}, bf16[288,768]{1,0:T(8,128)(2,1)S(1)}, u32[]{:S(2)}, u32[]{:S(2)}) %collective-permute-start.2) | collective-permute-done | bytes 442400 | tf_op jit(solution)/shard_map/ppermute | solution.py:34
  29.0 0.1 pad_maximum_fusion.refs_3_.refs_2_
  29.0 5.1 %collective-permute-start.17 = (bf16[576,768]{1,0:T(8,128)(2,1)S(1)}, bf16[576,768]{1,0:T(8,128)(2,1)S(1)}, u32[]{:S(2)}, u32[]{:S(2)}) collective-permute-start(bf16[576,768]{1,0:T(8,128)(2,1)S(1)} %pad_maximum_fusion.refs_3_.refs_2_), channel_id=1, source_target_pairs={{0,32},{32,0},{1,33},{33,1},{64,96},{96,64},{65,97},{97,65},{2,34}... | collective-permute-start | bytes 2654216 | tf_op jit(solution)/shard_map/ppermute | solution.py:34
  34.1 3.1 %collective-permute-start.9 = (bf16[576,768]{1,0:T(8,128)(2,1)S(1)}, bf16[576,768]{1,0:T(8,128)(2,1)S(1)}, u32[]{:S(2)}, u32[]{:S(2)}) collective-permute-start(bf16[576,768]{1,0:T(8,128)(2,1)S(1)} %pad_maximum_fusion.refs_3_.refs_2_), channel_id=1, source_target_pairs={{0,24},{32,38},{1,25},{33,39},{64,88},{96,102},{65,89},{97,103},{2... | collective-permute-start | bytes 2654216 | tf_op jit(solution)/shard_map/ppermute | solution.py:34
  37.2 0.0 collective-permute-done.20.refs_1_.refs_2_
  37.2 2.1 %collective-permute-start.6 = (bf16[576,768]{1,0:T(8,128)(2,1)S(1)}, bf16[576,768]{1,0:T(8,128)(2,1)S(1)}, u32[]{:S(2)}, u32[]{:S(2)}) collective-permute-start(bf16[576,768]{1,0:T(8,128)(2,1)S(1)} %pad_maximum_fusion.1.refs_4_.refs_3_), channel_id=1, source_target_pairs={{0,2},{32,56},{1,3},{33,57},{64,66},{96,120},{65,67},{97,121},{2,0... | collective-permute-start | bytes 2654216 | tf_op jit(solution)/shard_map/ppermute | solution.py:34
  39.3 0.0 collective-permute-done.18.refs_5_
  39.3 1.1 %collective-permute-start.5 = (bf16[576,768]{1,0:T(8,128)(2,1)S(1)}, bf16[576,768]{1,0:T(8,128)(2,1)S(1)}, u32[]{:S(2)}, u32[]{:S(2)}) collective-permute-start(bf16[576,768]{1,0:T(8,128)(2,1)S(1)} %pad_maximum_fusion.refs_3_.refs_2_), channel_id=1, source_target_pairs={{0,6},{32,40},{1,7},{33,41},{64,70},{96,104},{65,71},{97,105},{2,4... | collective-permute-start | bytes 2654216 | tf_op jit(solution)/shard_map/ppermute | solution.py:34
  40.4 0.0 collective-permute-done.11.refs_5_.refs_4_
  40.5 0.0 collective-permute-start.16
  40.5 0.0 collective-permute-done.17.refs_4_
  40.5 0.8 collective-permute-start.12
  41.2 13.4 %collective-permute-done.9.refs_4_.refs_3_ = bf16[576,768]{1,0:T(8,128)(2,1)S(1)} collective-permute-done((bf16[576,768]{1,0:T(8,128)(2,1)S(1)}, bf16[576,768]{1,0:T(8,128)(2,1)S(1)}, u32[]{:S(2)}, u32[]{:S(2)}) %collective-permute-start.9) | collective-permute-done | bytes 884768 | tf_op jit(solution)/shard_map/ppermute | solution.py:34
  54.6 1.6 %collective-permute-start.10 = (bf16[576,768]{1,0:T(8,128)(2,1)S(1)}, bf16[576,768]{1,0:T(8,128)(2,1)S(1)}, u32[]{:S(2)}, u32[]{:S(2)}) collective-permute-start(bf16[576,768]{1,0:T(8,128)(2,1)S(1)} %collective-permute-done.9.refs_4_.refs_3_), channel_id=1, source_target_pairs={{0,6},{32,40},{1,7},{33,41},{64,70},{96,104},{65,71},{97,105},{2,4... | collective-permute-start | bytes 2654216 | tf_op jit(solution)/shard_map/ppermute | solution.py:34
  56.2 1.2 %collective-permute-done.6.refs_5_.refs_4_ = bf16[576,768]{1,0:T(8,128)(2,1)S(1)} collective-permute-done((bf16[576,768]{1,0:T(8,128)(2,1)S(1)}, bf16[576,768]{1,0:T(8,128)(2,1)S(1)}, u32[]{:S(2)}, u32[]{:S(2)}) %collective-permute-start.6) | collective-permute-done | bytes 884768 | tf_op jit(solution)/shard_map/ppermute | solution.py:34
  57.4 3.9 %collective-permute-start.15 = (bf16[576,768]{1,0:T(8,128)(2,1)S(1)}, bf16[576,768]{1,0:T(8,128)(2,1)S(1)}, u32[]{:S(2)}, u32[]{:S(2)}) collective-permute-start(bf16[576,768]{1,0:T(8,128)(2,1)S(1)} %collective-permute-done.9.refs_4_.refs_3_), channel_id=1, source_target_pairs={{0,32},{32,0},{1,33},{33,1},{64,96},{96,64},{65,97},{97,65},{2,34}... | collective-permute-start | bytes 2654216 | tf_op jit(solution)/shard_map/ppermute | solution.py:34
  61.3 0.0 collective-permute-done.5.refs_4_.refs_3_
  61.3 0.1 collective-permute-start.8
  61.4 0.0 collective-permute-done.16.refs_7_.refs_6_
  61.4 0.4 collective-permute-start.7
  61.8 2.2 %pairs.11 = (f32[512,768]{1,0:T(8,128)S(1)}, f32[512,128]{1,0:T(8,128)S(1)}, f32[512,128]{1,0:T(8,128)S(1)}) custom-call(bf16[128,128]{1,0:T(8,128)(2,1)S(1)} %get-tuple-element.15.refs_0_, bf16[272,768]{1,0:T(8,128)(2,1)S(1)} %get-tuple-element.16.refs_1_.refs_2_, bf16[272,768]{1,0:T(8,128)(2,1)S(1)} %collective-permute-done.refs_2_.refs_3_, ...), custom_call_target="tpu_custom_call" | custom-call | flops 1610612736 | tf_op jit(solution)/shard_map/pairs/pallas_call | solution.py:185
  64.1 2.3 %pairs.12.refs_8_ = f32[512,768]{1,0:T(8,128)S(1)} custom-call(f32[512,128]{1,0:T(8,128)S(1)} %get-tuple-element.19.refs_0_, f32[512,128]{1,0:T(8,128)S(1)} %get-tuple-element.20.refs_1_, bf16[272,768]{1,0:T(8,128)(2,1)S(1)} %get-tuple-element.16.refs_1_.refs_2_, ...), custom_call_target="tpu_custom_call", output_to_operand_aliasing={{}: (6, {})} | custom-call | flops 1610612736 | tf_op jit(solution)/shard_map/pairs/pallas_call | solution.py:185
  66.4 4.6 %pairs.16 = (f32[512,768]{1,0:T(8,128)S(1)}, f32[512,128]{1,0:T(8,128)S(1)}, f32[512,128]{1,0:T(8,128)S(1)}) custom-call(bf16[128,128]{1,0:T(8,128)(2,1)S(1)} %get-tuple-element.15.refs_0_, bf16[544,768]{1,0:T(8,128)(2,1)S(1)} %collective-permute-done.20.refs_1_.refs_2_, bf16[576,768]{1,0:T(8,128)(2,1)S(1)} %pad_maximum_fusion.refs_3_.refs_2_, ...), custom_call_target="tpu_custom_call" | custom-call | flops 3221225472 | tf_op jit(solution)/shard_map/pairs/pallas_call | solution.py:185
  71.0 0.0 collective-permute-done.12.refs_9_.refs_4_
  71.0 0.2 collective-permute-start.14
  71.1 0.0 collective-permute-done.10.refs_8_.refs_3_
  71.1 1.2 %collective-permute-start.13 = (bf16[576,768]{1,0:T(8,128)(2,1)S(1)}, bf16[576,768]{1,0:T(8,128)(2,1)S(1)}, u32[]{:S(2)}, u32[]{:S(2)}) collective-permute-start(bf16[576,768]{1,0:T(8,128)(2,1)S(1)} %collective-permute-done.10.refs_8_.refs_3_), channel_id=1, source_target_pairs={{0,32},{32,0},{1,33},{33,1},{64,96},{96,64},{65,97},{97,65},{2,34}... | collective-permute-start | bytes 2654216 | tf_op jit(solution)/shard_map/ppermute | solution.py:34
  72.3 0.0 collective-permute-done.15.refs_6_.refs_5_
  72.3 4.5 %pairs.17.refs_7_ = f32[512,768]{1,0:T(8,128)S(1)} custom-call(f32[512,128]{1,0:T(8,128)S(1)} %get-tuple-element.22.refs_0_, f32[512,128]{1,0:T(8,128)S(1)} %get-tuple-element.23.refs_1_, bf16[544,768]{1,0:T(8,128)(2,1)S(1)} %collective-permute-done.20.refs_1_.refs_2_, ...), custom_call_target="tpu_custom_call", output_to_operand_aliasing={{}: (7, {})} | custom-call | flops 3221225472 | tf_op jit(solution)/shard_map/pairs/pallas_call | solution.py:185
  76.9 0.0 collective-permute-done.8.refs_7_.refs_6_
  76.9 0.0 collective-permute-done.7.refs_6_.refs_5_
  76.9 4.5 %pairs.18.refs_5_ = f32[512,768]{1,0:T(8,128)S(1)} custom-call(f32[512,128]{1,0:T(8,128)S(1)} %get-tuple-element.22.refs_0_, f32[512,128]{1,0:T(8,128)S(1)} %get-tuple-element.23.refs_1_, bf16[544,768]{1,0:T(8,128)(2,1)S(1)} %collective-permute-done.20.refs_1_.refs_2_, ...), custom_call_target="tpu_custom_call", output_to_operand_aliasing={{}: (7, {})} | custom-call | flops 3221225472 | tf_op jit(solution)/shard_map/pairs/pallas_call | solution.py:185
  81.4 2.2 %pairs.19.refs_5_ = f32[512,768]{1,0:T(8,128)S(1)} custom-call(f32[512,128]{1,0:T(8,128)S(1)} %get-tuple-element.22.refs_0_, f32[512,128]{1,0:T(8,128)S(1)} %get-tuple-element.23.refs_1_, bf16[544,768]{1,0:T(8,128)(2,1)S(1)} %collective-permute-done.20.refs_1_.refs_2_, ...), custom_call_target="tpu_custom_call", output_to_operand_aliasing={{}: (5, {})} | custom-call | flops 1610612736 | tf_op jit(solution)/shard_map/pairs/pallas_call | solution.py:185
  83.6 4.5 %pairs.13.refs_12_ = f32[512,768]{1,0:T(8,128)S(1)} custom-call(f32[512,128]{1,0:T(8,128)S(1)} %get-tuple-element.19.refs_0_, f32[512,128]{1,0:T(8,128)S(1)} %get-tuple-element.20.refs_1_, bf16[272,768]{1,0:T(8,128)(2,1)S(1)} %get-tuple-element.16.refs_1_.refs_2_, ...), custom_call_target="tpu_custom_call", output_to_operand_aliasing={{}: (8, {})} | custom-call | flops 3221225472 | tf_op jit(solution)/shard_map/pairs/pallas_call | solution.py:185
  88.2 0.0 collective-permute-done.14.refs_11_.refs_4_
  88.2 0.0 collective-permute-done.13.refs_10_.refs_3_
  88.2 1.2 %pairs.21 = f32[256,768]{1,0:T(8,128)S(1)} custom-call(f32[512,128]{1,0:T(8,128)S(1)} %get-tuple-element.22.refs_0_, f32[512,128]{1,0:T(8,128)S(1)} %get-tuple-element.23.refs_1_, bf16[544,768]{1,0:T(8,128)(2,1)S(1)} %collective-permute-done.20.refs_1_.refs_2_, bf16[576,768]{1,0:T(8,128)(2,1)S(1)} %collective-permute-done.13.refs_10_.refs_3_, ...), custom_call_target="tpu_custom_call" | custom-call | flops 805306368 | tf_op jit(solution)/shard_map/pairs/pallas_call | solution.py:185
  89.4 0.1 multiply_convert_fusion.1
  89.5 3.0 %collective-permute-start.21 = (f16[256,768]{1,0:T(8,128)(2,1)S(1)}, f16[256,768]{1,0:T(8,128)(2,1)S(1)}, u32[]{:S(2)}, u32[]{:S(2)}) collective-permute-start(f16[256,768]{1,0:T(8,128)(2,1)S(1)} %multiply_convert_fusion.1), channel_id=1, source_target_pairs={{0,1},{32,97},{1,0},{33,96},{64,65},{96,33},{65,64},{97,32},{2,3},... | collective-permute-start | bytes 1179656 | tf_op jit(solution)/shard_map/ppermute | solution.py:34
  92.6 4.1 %pairs.15 = f32[256,768]{1,0:T(8,128)S(1)} custom-call(f32[512,128]{1,0:T(8,128)S(1)} %get-tuple-element.19.refs_0_, f32[512,128]{1,0:T(8,128)S(1)} %get-tuple-element.20.refs_1_, bf16[272,768]{1,0:T(8,128)(2,1)S(1)} %get-tuple-element.16.refs_1_.refs_2_, bf16[272,768]{1,0:T(8,128)(2,1)S(1)} %collective-permute-done.refs_2_.refs_3_, ...), custom_call_target="tpu_custom_call" | custom-call | flops 3221225472 | tf_op jit(solution)/shard_map/pairs/pallas_call | solution.py:185
  96.7 0.1 multiply_convert_fusion.2
  96.7 0.1 collective-permute-start.19
  96.9 1.2 %pairs.20 = f32[256,768]{1,0:T(8,128)S(1)} custom-call(f32[512,128]{1,0:T(8,128)S(1)} %get-tuple-element.22.refs_0_, f32[512,128]{1,0:T(8,128)S(1)} %get-tuple-element.23.refs_1_, bf16[544,768]{1,0:T(8,128)(2,1)S(1)} %collective-permute-done.20.refs_1_.refs_2_, bf16[576,768]{1,0:T(8,128)(2,1)S(1)} %collective-permute-done.13.refs_10_.refs_3_, ...), custom_call_target="tpu_custom_call" | custom-call | flops 805306368 | tf_op jit(solution)/shard_map/pairs/pallas_call | solution.py:185
  98.1 0.0 collective-permute-done.21
  98.1 0.1 multiply_convert_fusion
  98.2 0.1 collective-permute-start.22
  98.3 4.1 %pairs.14 = f32[256,768]{1,0:T(8,128)S(1)} custom-call(f32[512,128]{1,0:T(8,128)S(1)} %get-tuple-element.19.refs_0_, f32[512,128]{1,0:T(8,128)S(1)} %get-tuple-element.20.refs_1_, bf16[272,768]{1,0:T(8,128)(2,1)S(1)} %get-tuple-element.16.refs_1_.refs_2_, bf16[272,768]{1,0:T(8,128)(2,1)S(1)} %collective-permute-done.refs_2_.refs_3_, ...), custom_call_target="tpu_custom_call" | custom-call | flops 3221225472 | tf_op jit(solution)/shard_map/pairs/pallas_call | solution.py:185
  102.5 5.3 %collective-permute-done.19 = f16[256,768]{1,0:T(8,128)(2,1)S(1)} collective-permute-done((f16[256,768]{1,0:T(8,128)(2,1)S(1)}, f16[256,768]{1,0:T(8,128)(2,1)S(1)}, u32[]{:S(2)}, u32[]{:S(2)}) %collective-permute-start.19) | collective-permute-done | bytes 393248 | tf_op jit(solution)/shard_map/ppermute | solution.py:34
  107.7 1.1 multiply_add_fusion
  (3 shorter events, 0.1 us)
Async XLA Ops:
  1.2 8.2 %collective-permute-start.3 = (bf16[144,768]{1,0:T(8,128)(2,1)S(1)}, bf16[144,768]{1,0:T(8,128)(2,1)S(1)}, u32[]{:S(2)}, u32[]{:S(2)}) collective-permute-start(bf16[144,768]{1,0:T(8,128)(2,1)S(1)} %get-tuple-element.18), channel_id=1, source_target_pairs={{0,24},{32,38},{1,25},{33,39},{64,88},{96,102},{65,89},{97,103},{2... | collective-permute-start | bytes 663560 | tf_op jit(solution)/shard_map/ppermute | solution.py:34
  5.8 8.2 %collective-permute-start = (bf16[272,768]{1,0:T(8,128)(2,1)S(1)}, bf16[272,768]{1,0:T(8,128)(2,1)S(1)}, u32[]{:S(2)}, u32[]{:S(2)}) collective-permute-start(bf16[272,768]{1,0:T(8,128)(2,1)S(1)} %get-tuple-element.16.refs_1_.refs_2_), channel_id=1, source_target_pairs={{0,1},{32,97},{1,0},{33,96},{64,65},{96,33},{65,64},{97,32},{2,3},... | collective-permute-start | bytes 1253384 | tf_op jit(solution)/shard_map/ppermute | solution.py:34
  9.4 7.5 %collective-permute-start.4 = (bf16[288,768]{1,0:T(8,128)(2,1)S(1)}, bf16[288,768]{1,0:T(8,128)(2,1)S(1)}, u32[]{:S(2)}, u32[]{:S(2)}) collective-permute-start(bf16[288,768]{1,0:T(8,128)(2,1)S(1)} %pad_maximum_fusion.4), channel_id=1, source_target_pairs={{0,6},{32,40},{1,7},{33,41},{64,70},{96,104},{65,71},{97,105},{2,4... | collective-permute-start | bytes 1327112 | tf_op jit(solution)/shard_map/ppermute | solution.py:34
  10.5 10.0 %collective-permute-start.1 = (bf16[144,768]{1,0:T(8,128)(2,1)S(1)}, bf16[144,768]{1,0:T(8,128)(2,1)S(1)}, u32[]{:S(2)}, u32[]{:S(2)}) collective-permute-start(bf16[144,768]{1,0:T(8,128)(2,1)S(1)} %get-tuple-element.17), channel_id=1, source_target_pairs={{0,8},{32,34},{1,9},{33,35},{64,72},{96,98},{65,73},{97,99},{2,10}... | collective-permute-start | bytes 663560 | tf_op jit(solution)/shard_map/ppermute | solution.py:34
  14.1 23.2 %collective-permute-start.20 = (bf16[544,768]{1,0:T(8,128)(2,1)S(1)}, bf16[544,768]{1,0:T(8,128)(2,1)S(1)}, u32[]{:S(2)}, u32[]{:S(2)}) collective-permute-start(bf16[544,768]{1,0:T(8,128)(2,1)S(1)} %pad_maximum_fusion.2), channel_id=1, source_target_pairs={{0,65},{32,33},{1,64},{33,32},{64,1},{96,97},{65,0},{97,96},{2,67}... | collective-permute-start | bytes 2506760 | tf_op jit(solution)/shard_map/ppermute | solution.py:34
  17.0 22.3 %collective-permute-start.18 = (bf16[576,768]{1,0:T(8,128)(2,1)S(1)}, bf16[576,768]{1,0:T(8,128)(2,1)S(1)}, u32[]{:S(2)}, u32[]{:S(2)}) collective-permute-start(bf16[576,768]{1,0:T(8,128)(2,1)S(1)} %pad_maximum_fusion.1.refs_4_.refs_3_), channel_id=1, source_target_pairs={{0,32},{32,0},{1,33},{33,1},{64,96},{96,64},{65,97},{97,65},{2,34}... | collective-permute-start | bytes 2654216 | tf_op jit(solution)/shard_map/ppermute | solution.py:34
  20.5 20.0 %collective-permute-start.11 = (bf16[576,768]{1,0:T(8,128)(2,1)S(1)}, bf16[576,768]{1,0:T(8,128)(2,1)S(1)}, u32[]{:S(2)}, u32[]{:S(2)}) collective-permute-start(bf16[576,768]{1,0:T(8,128)(2,1)S(1)} %pad_maximum_fusion.1.refs_4_.refs_3_), channel_id=1, source_target_pairs={{0,8},{32,34},{1,9},{33,35},{64,72},{96,98},{65,73},{97,99},{2,10}... | collective-permute-start | bytes 2654216 | tf_op jit(solution)/shard_map/ppermute | solution.py:34
  20.5 8.4 %collective-permute-start.2 = (bf16[288,768]{1,0:T(8,128)(2,1)S(1)}, bf16[288,768]{1,0:T(8,128)(2,1)S(1)}, u32[]{:S(2)}, u32[]{:S(2)}) collective-permute-start(bf16[288,768]{1,0:T(8,128)(2,1)S(1)} %pad_maximum_fusion.3), channel_id=1, source_target_pairs={{0,2},{32,56},{1,3},{33,57},{64,66},{96,120},{65,67},{97,121},{2,0... | collective-permute-start | bytes 1327112 | tf_op jit(solution)/shard_map/ppermute | solution.py:34
  29.0 11.4 %collective-permute-start.17 = (bf16[576,768]{1,0:T(8,128)(2,1)S(1)}, bf16[576,768]{1,0:T(8,128)(2,1)S(1)}, u32[]{:S(2)}, u32[]{:S(2)}) collective-permute-start(bf16[576,768]{1,0:T(8,128)(2,1)S(1)} %pad_maximum_fusion.refs_3_.refs_2_), channel_id=1, source_target_pairs={{0,32},{32,0},{1,33},{33,1},{64,96},{96,64},{65,97},{97,65},{2,34}... | collective-permute-start | bytes 2654216 | tf_op jit(solution)/shard_map/ppermute | solution.py:34
  34.1 20.5 %collective-permute-start.9 = (bf16[576,768]{1,0:T(8,128)(2,1)S(1)}, bf16[576,768]{1,0:T(8,128)(2,1)S(1)}, u32[]{:S(2)}, u32[]{:S(2)}) collective-permute-start(bf16[576,768]{1,0:T(8,128)(2,1)S(1)} %pad_maximum_fusion.refs_3_.refs_2_), channel_id=1, source_target_pairs={{0,24},{32,38},{1,25},{33,39},{64,88},{96,102},{65,89},{97,103},{2... | collective-permute-start | bytes 2654216 | tf_op jit(solution)/shard_map/ppermute | solution.py:34
  37.2 20.2 %collective-permute-start.6 = (bf16[576,768]{1,0:T(8,128)(2,1)S(1)}, bf16[576,768]{1,0:T(8,128)(2,1)S(1)}, u32[]{:S(2)}, u32[]{:S(2)}) collective-permute-start(bf16[576,768]{1,0:T(8,128)(2,1)S(1)} %pad_maximum_fusion.1.refs_4_.refs_3_), channel_id=1, source_target_pairs={{0,2},{32,56},{1,3},{33,57},{64,66},{96,120},{65,67},{97,121},{2,0... | collective-permute-start | bytes 2654216 | tf_op jit(solution)/shard_map/ppermute | solution.py:34
  39.3 22.0 %collective-permute-start.5 = (bf16[576,768]{1,0:T(8,128)(2,1)S(1)}, bf16[576,768]{1,0:T(8,128)(2,1)S(1)}, u32[]{:S(2)}, u32[]{:S(2)}) collective-permute-start(bf16[576,768]{1,0:T(8,128)(2,1)S(1)} %pad_maximum_fusion.refs_3_.refs_2_), channel_id=1, source_target_pairs={{0,6},{32,40},{1,7},{33,41},{64,70},{96,104},{65,71},{97,105},{2,4... | collective-permute-start | bytes 2654216 | tf_op jit(solution)/shard_map/ppermute | solution.py:34
  40.5 21.0 %collective-permute-start.16 = (bf16[576,768]{1,0:T(8,128)(2,1)S(1)}, bf16[576,768]{1,0:T(8,128)(2,1)S(1)}, u32[]{:S(2)}, u32[]{:S(2)}) collective-permute-start(bf16[576,768]{1,0:T(8,128)(2,1)S(1)} %collective-permute-done.11.refs_5_.refs_4_), channel_id=1, source_target_pairs={{0,32},{32,0},{1,33},{33,1},{64,96},{96,64},{65,97},{97,65},{2,34}... | collective-permute-start | bytes 2654216 | tf_op jit(solution)/shard_map/ppermute | solution.py:34
  40.5 30.5 %collective-permute-start.12 = (bf16[576,768]{1,0:T(8,128)(2,1)S(1)}, bf16[576,768]{1,0:T(8,128)(2,1)S(1)}, u32[]{:S(2)}, u32[]{:S(2)}) collective-permute-start(bf16[576,768]{1,0:T(8,128)(2,1)S(1)} %collective-permute-done.11.refs_5_.refs_4_), channel_id=1, source_target_pairs={{0,2},{32,56},{1,3},{33,57},{64,66},{96,120},{65,67},{97,121},{2,0... | collective-permute-start | bytes 2654216 | tf_op jit(solution)/shard_map/ppermute | solution.py:34
  54.6 16.5 %collective-permute-start.10 = (bf16[576,768]{1,0:T(8,128)(2,1)S(1)}, bf16[576,768]{1,0:T(8,128)(2,1)S(1)}, u32[]{:S(2)}, u32[]{:S(2)}) collective-permute-start(bf16[576,768]{1,0:T(8,128)(2,1)S(1)} %collective-permute-done.9.refs_4_.refs_3_), channel_id=1, source_target_pairs={{0,6},{32,40},{1,7},{33,41},{64,70},{96,104},{65,71},{97,105},{2,4... | collective-permute-start | bytes 2654216 | tf_op jit(solution)/shard_map/ppermute | solution.py:34
  57.4 14.9 %collective-permute-start.15 = (bf16[576,768]{1,0:T(8,128)(2,1)S(1)}, bf16[576,768]{1,0:T(8,128)(2,1)S(1)}, u32[]{:S(2)}, u32[]{:S(2)}) collective-permute-start(bf16[576,768]{1,0:T(8,128)(2,1)S(1)} %collective-permute-done.9.refs_4_.refs_3_), channel_id=1, source_target_pairs={{0,32},{32,0},{1,33},{33,1},{64,96},{96,64},{65,97},{97,65},{2,34}... | collective-permute-start | bytes 2654216 | tf_op jit(solution)/shard_map/ppermute | solution.py:34
  61.3 15.5 %collective-permute-start.8 = (bf16[576,768]{1,0:T(8,128)(2,1)S(1)}, bf16[576,768]{1,0:T(8,128)(2,1)S(1)}, u32[]{:S(2)}, u32[]{:S(2)}) collective-permute-start(bf16[576,768]{1,0:T(8,128)(2,1)S(1)} %collective-permute-done.6.refs_5_.refs_4_), channel_id=1, source_target_pairs={{0,32},{32,0},{1,33},{33,1},{64,96},{96,64},{65,97},{97,65},{2,34}... | collective-permute-start | bytes 2654216 | tf_op jit(solution)/shard_map/ppermute | solution.py:34
  61.4 15.5 %collective-permute-start.7 = (bf16[576,768]{1,0:T(8,128)(2,1)S(1)}, bf16[576,768]{1,0:T(8,128)(2,1)S(1)}, u32[]{:S(2)}, u32[]{:S(2)}) collective-permute-start(bf16[576,768]{1,0:T(8,128)(2,1)S(1)} %collective-permute-done.5.refs_4_.refs_3_), channel_id=1, source_target_pairs={{0,32},{32,0},{1,33},{33,1},{64,96},{96,64},{65,97},{97,65},{2,34}... | collective-permute-start | bytes 2654216 | tf_op jit(solution)/shard_map/ppermute | solution.py:34
  71.0 17.2 %collective-permute-start.14 = (bf16[576,768]{1,0:T(8,128)(2,1)S(1)}, bf16[576,768]{1,0:T(8,128)(2,1)S(1)}, u32[]{:S(2)}, u32[]{:S(2)}) collective-permute-start(bf16[576,768]{1,0:T(8,128)(2,1)S(1)} %collective-permute-done.12.refs_9_.refs_4_), channel_id=1, source_target_pairs={{0,32},{32,0},{1,33},{33,1},{64,96},{96,64},{65,97},{97,65},{2,34}... | collective-permute-start | bytes 2654216 | tf_op jit(solution)/shard_map/ppermute | solution.py:34
  71.1 17.1 %collective-permute-start.13 = (bf16[576,768]{1,0:T(8,128)(2,1)S(1)}, bf16[576,768]{1,0:T(8,128)(2,1)S(1)}, u32[]{:S(2)}, u32[]{:S(2)}) collective-permute-start(bf16[576,768]{1,0:T(8,128)(2,1)S(1)} %collective-permute-done.10.refs_8_.refs_3_), channel_id=1, source_target_pairs={{0,32},{32,0},{1,33},{33,1},{64,96},{96,64},{65,97},{97,65},{2,34}... | collective-permute-start | bytes 2654216 | tf_op jit(solution)/shard_map/ppermute | solution.py:34
  89.5 8.6 %collective-permute-start.21 = (f16[256,768]{1,0:T(8,128)(2,1)S(1)}, f16[256,768]{1,0:T(8,128)(2,1)S(1)}, u32[]{:S(2)}, u32[]{:S(2)}) collective-permute-start(f16[256,768]{1,0:T(8,128)(2,1)S(1)} %multiply_convert_fusion.1), channel_id=1, source_target_pairs={{0,1},{32,97},{1,0},{33,96},{64,65},{96,33},{65,64},{97,32},{2,3},... | collective-permute-start | bytes 1179656 | tf_op jit(solution)/shard_map/ppermute | solution.py:34
  96.7 11.0 %collective-permute-start.19 = (f16[256,768]{1,0:T(8,128)(2,1)S(1)}, f16[256,768]{1,0:T(8,128)(2,1)S(1)}, u32[]{:S(2)}, u32[]{:S(2)}) collective-permute-start(f16[256,768]{1,0:T(8,128)(2,1)S(1)} %multiply_convert_fusion.2), channel_id=1, source_target_pairs={{0,1},{32,97},{1,0},{33,96},{64,65},{96,33},{65,64},{97,32},{2,3},... | collective-permute-start | bytes 1179656 | tf_op jit(solution)/shard_map/ppermute | solution.py:34
  98.2 9.5 %collective-permute-start.22 = (f16[256,768]{1,0:T(8,128)(2,1)S(1)}, f16[256,768]{1,0:T(8,128)(2,1)S(1)}, u32[]{:S(2)}, u32[]{:S(2)}) collective-permute-start(f16[256,768]{1,0:T(8,128)(2,1)S(1)} %multiply_convert_fusion), channel_id=1, source_target_pairs={{0,65},{32,33},{1,64},{33,32},{64,1},{96,97},{65,0},{97,96},{2,67}... | collective-permute-start | bytes 1179656 | tf_op jit(solution)/shard_map/ppermute | solution.py:34

commit v3 on v2

--- a/solution.py
+++ b/solution.py
@@ -16,7 +16,7 @@
 LANES = 128
 LINK_SCALE = 16.0
 BLOCK = 256
-META = 16
+META = 8
 
 
 def position(x, z, y, core):
@@ -237,14 +237,17 @@
     near_sum = step(near_lookup, near, others[0], near_sum)
     both = [own + other for own, other in zip(arrived, others)]
     near_sum = step(near_lookup, near, both[1], near_sum)
-    far_sum, *far_lookup = step(table, far, both[0], None)
+    far_sum, *far_lookup = step(table, far, arrived[0], None)
     far_lookup = tuple(far_lookup)
-    far_sum = step(far_lookup, far, both[1], far_sum)
+    far_sum = step(far_lookup, far, others[0], far_sum)
+    far_sum = step(far_lookup, far, arrived[1], far_sum)
+    far_sum = step(far_lookup, far, others[1], far_sum)
     far_sum = step(far_lookup, far, both[2], far_sum)
+    near_part = step(near_lookup, near, both[2], near_sum, first=1, blocks=1, carry_first=1)
     far_sum = step(far_lookup, far, arrived[3], far_sum)
     last = step(far_lookup, far, others[3], far_sum, first=1, blocks=1, carry_first=1)
     relay = exchange(to_link(last), line_step(0))
-    near0 = step(near_lookup, near, both[2] + both[3], near_sum, first=1, blocks=1, carry_first=1)
+    near0 = step(near_lookup, near, both[3], near_part, first=1, blocks=1, carry_first=0)
     back0 = exchange(to_link(near0), line_step(0))
     near1 = step(far_lookup, far, others[3], far_sum, first=0, blocks=1, carry_first=0)
     back1 = exchange(to_link(near1 + from_link(relay)), line_step(1))

time: 109 us -> 105 us (0.963)
  waiting for transfers between devices: 32.6 us -> 29.1 us
    ppermute x23, waiting for transfers between devices: 32.6 us -> 29.1 us  [exchange(): return lax.ppermute(value, AXES, pairs)]
    pallas_call x11 -> x14, Pallas kernels: 35.6 us -> 36.1 us  [pairs(): pl.pallas_call(functools.partial(pair_body, units, len(line), first, bloc...]
  transfers between devices with their start and end apart: 23 -> 23, of which waited for: 7 -> 9; matrix products, arithmetic and copies ran while one was open for 0% -> 0% of each run, Pallas kernels for 32% -> 33%
where the time goes in v3:
time: 105 us
  Pallas kernels  37.2 us (35%)
  starting transfers between devices  36.9 us (35%)
  waiting for transfers between devices  29.1 us (28%)
  other arithmetic  1.58 us (2%)
    ppermute x23, starting transfers between devices, exchange(): return lax.ppermute(value, AXES, pairs)  36.9 us
    pallas_call x14, Pallas kernels, pairs(): pl.pallas_call(functools.partial(pair_body, units, len(line), first, bloc...  36.1 us
    ppermute x23, waiting for transfers between devices, exchange(): return lax.ppermute(value, AXES, pairs)  29.1 us
  transfers between devices with their start and end apart: 23, of which 9 were waited for; matrix products, arithmetic and copies ran while one was open for 0% of the time, Pallas kernels for 33%

profile of v3, /device:TPU:1, one launch (start us, length us, event | category | flops | bytes accessed | tf_op | source)
XLA Modules:
  0.0 105.1 jit_solution(9138586964046753625)
XLA Ops:
  0.0 1.2 %pack.1 = (bf16[264,768]{1,0:T(8,128)(2,1)S(1)}, bf16[136,768]{1,0:T(8,128)(2,1)S(1)}, bf16[136,768]{1,0:T(8,128)(2,1)S(1)}, bf16[128,128]{1,0:T(8,128)(2,1)S(1)}) custom-call(bf16[256,768]{1,0:T(8,128)(2,1)} %rows_ref.1, s32[2,128]{1,0:T(2,128)} %bitcast.2, s32[2,128]{1,0:T(2,128)} %bitcast.3, s32[109,109]{1,0:T(8,128)} %mask_ref.1), custom_call_target="tpu_custom_call" | custom-call | tf_op jit(solution)/shard_map/pack/pallas_call | solution.py:84
  1.2 3.6 %collective-permute-start = (bf16[264,768]{1,0:T(8,128)(2,1)S(1)}, bf16[264,768]{1,0:T(8,128)(2,1)S(1)}, u32[]{:S(2)}, u32[]{:S(2)}) collective-permute-start(bf16[264,768]{1,0:T(8,128)(2,1)S(1)} %get-tuple-element.16.refs_1_.refs_2_), channel_id=1, source_target_pairs={{0,1},{32,97},{1,0},{33,96},{64,65},{96,33},{65,64},{97,32},{2,3},... | collective-permute-start | bytes 1216520 | tf_op jit(solution)/shard_map/ppermute | solution.py:34
  4.8 3.8 %collective-permute-start.3 = (bf16[136,768]{1,0:T(8,128)(2,1)S(1)}, bf16[136,768]{1,0:T(8,128)(2,1)S(1)}, u32[]{:S(2)}, u32[]{:S(2)}) collective-permute-start(bf16[136,768]{1,0:T(8,128)(2,1)S(1)} %get-tuple-element.18), channel_id=1, source_target_pairs={{0,24},{32,38},{1,25},{33,39},{64,88},{96,102},{65,89},{97,103},{2... | collective-permute-start | bytes 626696 | tf_op jit(solution)/shard_map/ppermute | solution.py:34
  8.6 3.2 %collective-permute-done.3 = bf16[136,768]{1,0:T(8,128)(2,1)S(1)} collective-permute-done((bf16[136,768]{1,0:T(8,128)(2,1)S(1)}, bf16[136,768]{1,0:T(8,128)(2,1)S(1)}, u32[]{:S(2)}, u32[]{:S(2)}) %collective-permute-start.3) | collective-permute-done | bytes 208928 | tf_op jit(solution)/shard_map/ppermute | solution.py:34
  11.8 1.3 %collective-permute-start.4 = (bf16[272,768]{1,0:T(8,128)(2,1)S(1)}, bf16[272,768]{1,0:T(8,128)(2,1)S(1)}, u32[]{:S(2)}, u32[]{:S(2)}) collective-permute-start(bf16[272,768]{1,0:T(8,128)(2,1)S(1)} %pad_maximum_fusion.4), channel_id=1, source_target_pairs={{0,6},{32,40},{1,7},{33,41},{64,70},{96,104},{65,71},{97,105},{2,4... | collective-permute-start | bytes 1253384 | tf_op jit(solution)/shard_map/ppermute | solution.py:34
  13.1 0.0 collective-permute-start.1
  13.1 0.0 collective-permute-done.refs_2_.refs_3_
  13.1 0.1 pad_maximum_fusion.2
  13.1 0.1 collective-permute-start.20
  13.2 4.8 %collective-permute-done.1 = bf16[136,768]{1,0:T(8,128)(2,1)S(1)} collective-permute-done((bf16[136,768]{1,0:T(8,128)(2,1)S(1)}, bf16[136,768]{1,0:T(8,128)(2,1)S(1)}, u32[]{:S(2)}, u32[]{:S(2)}) %collective-permute-start.1) | collective-permute-done | bytes 208928 | tf_op jit(solution)/shard_map/ppermute | solution.py:34
  18.1 1.9 %collective-permute-start.2 = (bf16[272,768]{1,0:T(8,128)(2,1)S(1)}, bf16[272,768]{1,0:T(8,128)(2,1)S(1)}, u32[]{:S(2)}, u32[]{:S(2)}) collective-permute-start(bf16[272,768]{1,0:T(8,128)(2,1)S(1)} %pad_maximum_fusion.3), channel_id=1, source_target_pairs={{0,2},{32,56},{1,3},{33,57},{64,66},{96,120},{65,67},{97,121},{2,0... | collective-permute-start | bytes 1253384 | tf_op jit(solution)/shard_map/ppermute | solution.py:34
  20.0 0.0 collective-permute-done.4
  20.0 0.1 pad_maximum_fusion.1.refs_4_.refs_3_
  20.0 2.0 %collective-permute-start.18 = (bf16[544,768]{1,0:T(8,128)(2,1)S(1)}, bf16[544,768]{1,0:T(8,128)(2,1)S(1)}, u32[]{:S(2)}, u32[]{:S(2)}) collective-permute-start(bf16[544,768]{1,0:T(8,128)(2,1)S(1)} %pad_maximum_fusion.1.refs_4_.refs_3_), channel_id=1, source_target_pairs={{0,32},{32,0},{1,33},{33,1},{64,96},{96,64},{65,97},{97,65},{2,34}... | collective-permute-start | bytes 2506760 | tf_op jit(solution)/shard_map/ppermute | solution.py:34
  22.0 1.7 %collective-permute-start.11 = (bf16[544,768]{1,0:T(8,128)(2,1)S(1)}, bf16[544,768]{1,0:T(8,128)(2,1)S(1)}, u32[]{:S(2)}, u32[]{:S(2)}) collective-permute-start(bf16[544,768]{1,0:T(8,128)(2,1)S(1)} %pad_maximum_fusion.1.refs_4_.refs_3_), channel_id=1, source_target_pairs={{0,8},{32,34},{1,9},{33,35},{64,72},{96,98},{65,73},{97,99},{2,10}... | collective-permute-start | bytes 2506760 | tf_op jit(solution)/shard_map/ppermute | solution.py:34
  23.7 2.8 %collective-permute-done.2 = bf16[272,768]{1,0:T(8,128)(2,1)S(1)} collective-permute-done((bf16[272,768]{1,0:T(8,128)(2,1)S(1)}, bf16[272,768]{1,0:T(8,128)(2,1)S(1)}, u32[]{:S(2)}, u32[]{:S(2)}) %collective-permute-start.2) | collective-permute-done | bytes 417824 | tf_op jit(solution)/shard_map/ppermute | solution.py:34
  26.5 0.1 pad_maximum_fusion.refs_3_.refs_2_
  26.6 7.9 %collective-permute-start.17 = (bf16[544,768]{1,0:T(8,128)(2,1)S(1)}, bf16[544,768]{1,0:T(8,128)(2,1)S(1)}, u32[]{:S(2)}, u32[]{:S(2)}) collective-permute-start(bf16[544,768]{1,0:T(8,128)(2,1)S(1)} %pad_maximum_fusion.refs_3_.refs_2_), channel_id=1, source_target_pairs={{0,32},{32,0},{1,33},{33,1},{64,96},{96,64},{65,97},{97,65},{2,34}... | collective-permute-start | bytes 2506760 | tf_op jit(solution)/shard_map/ppermute | solution.py:34
  34.5 1.0 collective-permute-start.9
  35.4 0.0 collective-permute-done.20.refs_1_.refs_2_
  35.4 2.5 %collective-permute-start.6 = (bf16[544,768]{1,0:T(8,128)(2,1)S(1)}, bf16[544,768]{1,0:T(8,128)(2,1)S(1)}, u32[]{:S(2)}, u32[]{:S(2)}) collective-permute-start(bf16[544,768]{1,0:T(8,128)(2,1)S(1)} %pad_maximum_fusion.1.refs_4_.refs_3_), channel_id=1, source_target_pairs={{0,2},{32,56},{1,3},{33,57},{64,66},{96,120},{65,67},{97,121},{2,0... | collective-permute-start | bytes 2506760 | tf_op jit(solution)/shard_map/ppermute | solution.py:34
  37.9 0.0 collective-permute-done.18.refs_5_.refs_4_
  37.9 0.2 collective-permute-done.11.refs_5_.refs_4_
  38.1 0.6 collective-permute-start.16
  38.6 2.4 %collective-permute-start.12 = (bf16[544,768]{1,0:T(8,128)(2,1)S(1)}, bf16[544,768]{1,0:T(8,128)(2,1)S(1)}, u32[]{:S(2)}, u32[]{:S(2)}) collective-permute-start(bf16[544,768]{1,0:T(8,128)(2,1)S(1)} %collective-permute-done.11.refs_5_.refs_4_), channel_id=1, source_target_pairs={{0,2},{32,56},{1,3},{33,57},{64,66},{96,120},{65,67},{97,121},{2,0... | collective-permute-start | bytes 2506760 | tf_op jit(solution)/shard_map/ppermute | solution.py:34
  41.0 11.9 %collective-permute-done.9.refs_4_.refs_3_ = bf16[544,768]{1,0:T(8,128)(2,1)S(1)} collective-permute-done((bf16[544,768]{1,0:T(8,128)(2,1)S(1)}, bf16[544,768]{1,0:T(8,128)(2,1)S(1)}, u32[]{:S(2)}, u32[]{:S(2)}) %collective-permute-start.9) | collective-permute-done | bytes 835616 | tf_op jit(solution)/shard_map/ppermute | solution.py:34
  52.9 2.5 %collective-permute-start.10 = (bf16[544,768]{1,0:T(8,128)(2,1)S(1)}, bf16[544,768]{1,0:T(8,128)(2,1)S(1)}, u32[]{:S(2)}, u32[]{:S(2)}) collective-permute-start(bf16[544,768]{1,0:T(8,128)(2,1)S(1)} %collective-permute-done.9.refs_4_.refs_3_), channel_id=1, source_target_pairs={{0,6},{32,40},{1,7},{33,41},{64,70},{96,104},{65,71},{97,105},{2,4... | collective-permute-start | bytes 2506760 | tf_op jit(solution)/shard_map/ppermute | solution.py:34
  55.4 1.2 %collective-permute-done.6.refs_5_.refs_4_ = bf16[544,768]{1,0:T(8,128)(2,1)S(1)} collective-permute-done((bf16[544,768]{1,0:T(8,128)(2,1)S(1)}, bf16[544,768]{1,0:T(8,128)(2,1)S(1)}, u32[]{:S(2)}, u32[]{:S(2)}) %collective-permute-start.6) | collective-permute-done | bytes 835616 | tf_op jit(solution)/shard_map/ppermute | solution.py:34
  56.5 0.8 collective-permute-start.15
  57.3 2.3 %pairs.14 = (f32[512,768]{1,0:T(8,128)S(1)}, f32[512,128]{1,0:T(8,128)S(1)}, f32[512,128]{1,0:T(8,128)S(1)}) custom-call(bf16[128,128]{1,0:T(8,128)(2,1)S(1)} %get-tuple-element.15.refs_0_, bf16[264,768]{1,0:T(8,128)(2,1)S(1)} %get-tuple-element.16.refs_1_.refs_2_, bf16[264,768]{1,0:T(8,128)(2,1)S(1)} %collective-permute-done.refs_2_.refs_3_, ...), custom_call_target="tpu_custom_call" | custom-call | flops 1610612736 | tf_op jit(solution)/shard_map/pairs/pallas_call | solution.py:185
  59.6 2.3 %pairs.20 = (f32[512,768]{1,0:T(8,128)S(1)}, f32[512,128]{1,0:T(8,128)S(1)}, f32[512,128]{1,0:T(8,128)S(1)}) custom-call(bf16[128,128]{1,0:T(8,128)(2,1)S(1)} %get-tuple-element.15.refs_0_, bf16[528,768]{1,0:T(8,128)(2,1)S(1)} %collective-permute-done.20.refs_1_.refs_2_, bf16[544,768]{1,0:T(8,128)(2,1)S(1)} %pad_maximum_fusion.refs_3_.refs_2_, ...), custom_call_target="tpu_custom_call" | custom-call | flops 1610612736 | tf_op jit(solution)/shard_map/pairs/pallas_call | solution.py:185
  61.9 0.1 collective-permute-start.8
  62.0 0.5 collective-permute-start.7
  62.5 2.2 %pairs.21.refs_5_ = f32[512,768]{1,0:T(8,128)S(1)} custom-call(f32[512,128]{1,0:T(8,128)S(1)} %get-tuple-element.22.refs_0_, f32[512,128]{1,0:T(8,128)S(1)} %get-tuple-element.23.refs_1_, bf16[528,768]{1,0:T(8,128)(2,1)S(1)} %collective-permute-done.20.refs_1_.refs_2_, ...), custom_call_target="tpu_custom_call", output_to_operand_aliasing={{}: (5, {})} | custom-call | flops 1610612736 | tf_op jit(solution)/shard_map/pairs/pallas_call | solution.py:185
  64.7 2.3 %pairs.22.refs_5_ = f32[512,768]{1,0:T(8,128)S(1)} custom-call(f32[512,128]{1,0:T(8,128)S(1)} %get-tuple-element.22.refs_0_, f32[512,128]{1,0:T(8,128)S(1)} %get-tuple-element.23.refs_1_, bf16[528,768]{1,0:T(8,128)(2,1)S(1)} %collective-permute-done.20.refs_1_.refs_2_, ...), custom_call_target="tpu_custom_call", output_to_operand_aliasing={{}: (5, {})} | custom-call | flops 1610612736 | tf_op jit(solution)/shard_map/pairs/pallas_call | solution.py:185
  67.0 2.2 %pairs.15.refs_8_ = f32[512,768]{1,0:T(8,128)S(1)} custom-call(f32[512,128]{1,0:T(8,128)S(1)} %get-tuple-element.19.refs_0_, f32[512,128]{1,0:T(8,128)S(1)} %get-tuple-element.20.refs_1_, bf16[264,768]{1,0:T(8,128)(2,1)S(1)} %get-tuple-element.16.refs_1_.refs_2_, ...), custom_call_target="tpu_custom_call", output_to_operand_aliasing={{}: (6, {})} | custom-call | flops 1610612736 | tf_op jit(solution)/shard_map/pairs/pallas_call | solution.py:185
  69.2 0.0 collective-permute-done.12.refs_9_.refs_5_.refs_4_
  69.2 0.4 collective-permute-start.14
  69.6 0.0 collective-permute-done.10.refs_8_.refs_4_.refs_3_
  69.6 0.9 collective-permute-start.13
  70.5 0.0 collective-permute-done.15.refs_6_.refs_3_
  70.6 2.3 %pairs.23.refs_7_ = f32[512,768]{1,0:T(8,128)S(1)} custom-call(f32[512,128]{1,0:T(8,128)S(1)} %get-tuple-element.22.refs_0_, f32[512,128]{1,0:T(8,128)S(1)} %get-tuple-element.23.refs_1_, bf16[528,768]{1,0:T(8,128)(2,1)S(1)} %collective-permute-done.20.refs_1_.refs_2_, ...), custom_call_target="tpu_custom_call", output_to_operand_aliasing={{}: (5, {})} | custom-call | flops 1610612736 | tf_op jit(solution)/shard_map/pairs/pallas_call | solution.py:185
  72.9 4.6 %pairs.16.refs_12_.refs_8_ = f32[512,768]{1,0:T(8,128)S(1)} custom-call(f32[512,128]{1,0:T(8,128)S(1)} %get-tuple-element.19.refs_0_, f32[512,128]{1,0:T(8,128)S(1)} %get-tuple-element.20.refs_1_, bf16[264,768]{1,0:T(8,128)(2,1)S(1)} %get-tuple-element.16.refs_1_.refs_2_, ...), custom_call_target="tpu_custom_call", output_to_operand_aliasing={{}: (8, {})} | custom-call | flops 3221225472 | tf_op jit(solution)/shard_map/pairs/pallas_call | solution.py:185
  77.4 0.0 collective-permute-done.8.refs_7_.refs_6_
  77.4 0.0 collective-permute-done.7.refs_6_.refs_5_
  77.4 2.2 %pairs.18.refs_8_ = f32[256,768]{1,0:T(8,128)S(1)} custom-call(f32[512,128]{1,0:T(8,128)S(1)} %get-tuple-element.19.refs_0_, f32[512,128]{1,0:T(8,128)S(1)} %get-tuple-element.20.refs_1_, bf16[264,768]{1,0:T(8,128)(2,1)S(1)} %get-tuple-element.16.refs_1_.refs_2_, bf16[264,768]{1,0:T(8,128)(2,1)S(1)} %collective-permute-done.refs_2_.refs_3_, ...), custom_call_target="tpu_custom_call" | custom-call | flops 1610612736 | tf_op jit(solution)/shard_map/pairs/pallas_call | solution.py:185
  79.6 4.6 %pairs.24.refs_5_ = f32[512,768]{1,0:T(8,128)S(1)} custom-call(f32[512,128]{1,0:T(8,128)S(1)} %get-tuple-element.22.refs_0_, f32[512,128]{1,0:T(8,128)S(1)} %get-tuple-element.23.refs_1_, bf16[528,768]{1,0:T(8,128)(2,1)S(1)} %collective-permute-done.20.refs_1_.refs_2_, ...), custom_call_target="tpu_custom_call", output_to_operand_aliasing={{}: (7, {})} | custom-call | flops 3221225472 | tf_op jit(solution)/shard_map/pairs/pallas_call | solution.py:185
  84.2 2.3 %pairs.25.refs_5_ = f32[512,768]{1,0:T(8,128)S(1)} custom-call(f32[512,128]{1,0:T(8,128)S(1)} %get-tuple-element.22.refs_0_, f32[512,128]{1,0:T(8,128)S(1)} %get-tuple-element.23.refs_1_, bf16[528,768]{1,0:T(8,128)(2,1)S(1)} %collective-permute-done.20.refs_1_.refs_2_, ...), custom_call_target="tpu_custom_call", output_to_operand_aliasing={{}: (5, {})} | custom-call | flops 1610612736 | tf_op jit(solution)/shard_map/pairs/pallas_call | solution.py:185
  86.5 0.0 collective-permute-done.14.refs_11_.refs_7_.refs_4_
  86.5 0.0 collective-permute-done.13.refs_10_.refs_6_.refs_3_
  86.5 1.3 %pairs.27 = f32[256,768]{1,0:T(8,128)S(1)} custom-call(f32[512,128]{1,0:T(8,128)S(1)} %get-tuple-element.22.refs_0_, f32[512,128]{1,0:T(8,128)S(1)} %get-tuple-element.23.refs_1_, bf16[528,768]{1,0:T(8,128)(2,1)S(1)} %collective-permute-done.20.refs_1_.refs_2_, bf16[544,768]{1,0:T(8,128)(2,1)S(1)} %collective-permute-done.13.refs_10_.refs_6_.refs_3_, ...), custom_call_target="tpu_custom_call" | custom-call | flops 805306368 | tf_op jit(solution)/shard_map/pairs/pallas_call | solution.py:185
  87.8 0.1 multiply_convert_fusion.1
  87.9 2.3 %collective-permute-start.21 = (f16[256,768]{1,0:T(8,128)(2,1)S(1)}, f16[256,768]{1,0:T(8,128)(2,1)S(1)}, u32[]{:S(2)}, u32[]{:S(2)}) collective-permute-start(f16[256,768]{1,0:T(8,128)(2,1)S(1)} %multiply_convert_fusion.1), channel_id=1, source_target_pairs={{0,1},{32,97},{1,0},{33,96},{64,65},{96,33},{65,64},{97,32},{2,3},... | collective-permute-start | bytes 1179656 | tf_op jit(solution)/shard_map/ppermute | solution.py:34
  90.1 2.2 %pairs.19 = f32[256,768]{1,0:T(8,128)S(1)} custom-call(f32[512,128]{1,0:T(8,128)S(1)} %get-tuple-element.19.refs_0_, f32[512,128]{1,0:T(8,128)S(1)} %get-tuple-element.20.refs_1_, bf16[264,768]{1,0:T(8,128)(2,1)S(1)} %get-tuple-element.16.refs_1_.refs_2_, bf16[264,768]{1,0:T(8,128)(2,1)S(1)} %collective-permute-done.refs_2_.refs_3_, ...), custom_call_target="tpu_custom_call", output_to_operand_aliasing={{}: (8, {})} | custom-call | flops 1610612736 | tf_op jit(solution)/shard_map/pairs/pallas_call | solution.py:185
  92.4 0.1 multiply_convert_fusion.2
  92.4 0.9 collective-permute-start.19
  93.3 1.3 %pairs.26 = f32[256,768]{1,0:T(8,128)S(1)} custom-call(f32[512,128]{1,0:T(8,128)S(1)} %get-tuple-element.22.refs_0_, f32[512,128]{1,0:T(8,128)S(1)} %get-tuple-element.23.refs_1_, bf16[528,768]{1,0:T(8,128)(2,1)S(1)} %collective-permute-done.20.refs_1_.refs_2_, bf16[544,768]{1,0:T(8,128)(2,1)S(1)} %collective-permute-done.13.refs_10_.refs_6_.refs_3_, ...), custom_call_target="tpu_custom_call" | custom-call | flops 805306368 | tf_op jit(solution)/shard_map/pairs/pallas_call | solution.py:185
  94.6 1.5 %collective-permute-done.21 = f16[256,768]{1,0:T(8,128)(2,1)S(1)} collective-permute-done((f16[256,768]{1,0:T(8,128)(2,1)S(1)}, f16[256,768]{1,0:T(8,128)(2,1)S(1)}, u32[]{:S(2)}, u32[]{:S(2)}) %collective-permute-start.21) | collective-permute-done | bytes 393248 | tf_op jit(solution)/shard_map/ppermute | solution.py:34
  96.0 0.2 multiply_convert_fusion
  96.2 0.1 collective-permute-start.22
  96.3 4.1 %pairs.17 = f32[256,768]{1,0:T(8,128)S(1)} custom-call(f32[512,128]{1,0:T(8,128)S(1)} %get-tuple-element.19.refs_0_, f32[512,128]{1,0:T(8,128)S(1)} %get-tuple-element.20.refs_1_, bf16[264,768]{1,0:T(8,128)(2,1)S(1)} %get-tuple-element.16.refs_1_.refs_2_, bf16[264,768]{1,0:T(8,128)(2,1)S(1)} %collective-permute-done.refs_2_.refs_3_, ...), custom_call_target="tpu_custom_call" | custom-call | flops 3221225472 | tf_op jit(solution)/shard_map/pairs/pallas_call | solution.py:185
  100.4 0.3 collective-permute-done.19
  100.7 3.3 %collective-permute-done.22 = f16[256,768]{1,0:T(8,128)(2,1)S(1)} collective-permute-done((f16[256,768]{1,0:T(8,128)(2,1)S(1)}, f16[256,768]{1,0:T(8,128)(2,1)S(1)}, u32[]{:S(2)}, u32[]{:S(2)}) %collective-permute-start.22) | collective-permute-done | bytes 393248 | tf_op jit(solution)/shard_map/ppermute | solution.py:34
  104.0 1.1 %multiply_add_fusion = f32[256,768]{1,0:T(8,128)} fusion(f16[256,768]{1,0:T(8,128)(2,1)S(1)} %collective-permute-done.22, f32[256,768]{1,0:T(8,128)S(1)} %pairs.17, f16[256,768]{1,0:T(8,128)(2,1)S(1)} %collective-permute-done.19), kind=kLoop, calls=%fused_computation.3 | loop fusion | flops 1179648 | bytes 2359296 | tf_op jit(solution)/shard_map/add | solution.py:255
  (6 shorter events, 0.1 us)
Async XLA Ops:
  1.2 11.9 %collective-permute-start = (bf16[264,768]{1,0:T(8,128)(2,1)S(1)}, bf16[264,768]{1,0:T(8,128)(2,1)S(1)}, u32[]{:S(2)}, u32[]{:S(2)}) collective-permute-start(bf16[264,768]{1,0:T(8,128)(2,1)S(1)} %get-tuple-element.16.refs_1_.refs_2_), channel_id=1, source_target_pairs={{0,1},{32,97},{1,0},{33,96},{64,65},{96,33},{65,64},{97,32},{2,3},... | collective-permute-start | bytes 1216520 | tf_op jit(solution)/shard_map/ppermute | solution.py:34
  4.8 6.9 %collective-permute-start.3 = (bf16[136,768]{1,0:T(8,128)(2,1)S(1)}, bf16[136,768]{1,0:T(8,128)(2,1)S(1)}, u32[]{:S(2)}, u32[]{:S(2)}) collective-permute-start(bf16[136,768]{1,0:T(8,128)(2,1)S(1)} %get-tuple-element.18), channel_id=1, source_target_pairs={{0,24},{32,38},{1,25},{33,39},{64,88},{96,102},{65,89},{97,103},{2... | collective-permute-start | bytes 626696 | tf_op jit(solution)/shard_map/ppermute | solution.py:34
  11.8 8.2 %collective-permute-start.4 = (bf16[272,768]{1,0:T(8,128)(2,1)S(1)}, bf16[272,768]{1,0:T(8,128)(2,1)S(1)}, u32[]{:S(2)}, u32[]{:S(2)}) collective-permute-start(bf16[272,768]{1,0:T(8,128)(2,1)S(1)} %pad_maximum_fusion.4), channel_id=1, source_target_pairs={{0,6},{32,40},{1,7},{33,41},{64,70},{96,104},{65,71},{97,105},{2,4... | collective-permute-start | bytes 1253384 | tf_op jit(solution)/shard_map/ppermute | solution.py:34
  13.1 4.9 %collective-permute-start.1 = (bf16[136,768]{1,0:T(8,128)(2,1)S(1)}, bf16[136,768]{1,0:T(8,128)(2,1)S(1)}, u32[]{:S(2)}, u32[]{:S(2)}) collective-permute-start(bf16[136,768]{1,0:T(8,128)(2,1)S(1)} %get-tuple-element.17), channel_id=1, source_target_pairs={{0,8},{32,34},{1,9},{33,35},{64,72},{96,98},{65,73},{97,99},{2,10}... | collective-permute-start | bytes 626696 | tf_op jit(solution)/shard_map/ppermute | solution.py:34
  13.1 22.3 %collective-permute-start.20 = (bf16[528,768]{1,0:T(8,128)(2,1)S(1)}, bf16[528,768]{1,0:T(8,128)(2,1)S(1)}, u32[]{:S(2)}, u32[]{:S(2)}) collective-permute-start(bf16[528,768]{1,0:T(8,128)(2,1)S(1)} %pad_maximum_fusion.2), channel_id=1, source_target_pairs={{0,65},{32,33},{1,64},{33,32},{64,1},{96,97},{65,0},{97,96},{2,67}... | collective-permute-start | bytes 2433032 | tf_op jit(solution)/shard_map/ppermute | solution.py:34
  18.1 8.5 %collective-permute-start.2 = (bf16[272,768]{1,0:T(8,128)(2,1)S(1)}, bf16[272,768]{1,0:T(8,128)(2,1)S(1)}, u32[]{:S(2)}, u32[]{:S(2)}) collective-permute-start(bf16[272,768]{1,0:T(8,128)(2,1)S(1)} %pad_maximum_fusion.3), channel_id=1, source_target_pairs={{0,2},{32,56},{1,3},{33,57},{64,66},{96,120},{65,67},{97,121},{2,0... | collective-permute-start | bytes 1253384 | tf_op jit(solution)/shard_map/ppermute | solution.py:34
  20.0 17.9 %collective-permute-start.18 = (bf16[544,768]{1,0:T(8,128)(2,1)S(1)}, bf16[544,768]{1,0:T(8,128)(2,1)S(1)}, u32[]{:S(2)}, u32[]{:S(2)}) collective-permute-start(bf16[544,768]{1,0:T(8,128)(2,1)S(1)} %pad_maximum_fusion.1.refs_4_.refs_3_), channel_id=1, source_target_pairs={{0,32},{32,0},{1,33},{33,1},{64,96},{96,64},{65,97},{97,65},{2,34}... | collective-permute-start | bytes 2506760 | tf_op jit(solution)/shard_map/ppermute | solution.py:34
  22.0 16.0 %collective-permute-start.11 = (bf16[544,768]{1,0:T(8,128)(2,1)S(1)}, bf16[544,768]{1,0:T(8,128)(2,1)S(1)}, u32[]{:S(2)}, u32[]{:S(2)}) collective-permute-start(bf16[544,768]{1,0:T(8,128)(2,1)S(1)} %pad_maximum_fusion.1.refs_4_.refs_3_), channel_id=1, source_target_pairs={{0,8},{32,34},{1,9},{33,35},{64,72},{96,98},{65,73},{97,99},{2,10}... | collective-permute-start | bytes 2506760 | tf_op jit(solution)/shard_map/ppermute | solution.py:34
  26.6 12.1 %collective-permute-start.17 = (bf16[544,768]{1,0:T(8,128)(2,1)S(1)}, bf16[544,768]{1,0:T(8,128)(2,1)S(1)}, u32[]{:S(2)}, u32[]{:S(2)}) collective-permute-start(bf16[544,768]{1,0:T(8,128)(2,1)S(1)} %pad_maximum_fusion.refs_3_.refs_2_), channel_id=1, source_target_pairs={{0,32},{32,0},{1,33},{33,1},{64,96},{96,64},{65,97},{97,65},{2,34}... | collective-permute-start | bytes 2506760 | tf_op jit(solution)/shard_map/ppermute | solution.py:34
  34.5 18.4 %collective-permute-start.9 = (bf16[544,768]{1,0:T(8,128)(2,1)S(1)}, bf16[544,768]{1,0:T(8,128)(2,1)S(1)}, u32[]{:S(2)}, u32[]{:S(2)}) collective-permute-start(bf16[544,768]{1,0:T(8,128)(2,1)S(1)} %pad_maximum_fusion.refs_3_.refs_2_), channel_id=1, source_target_pairs={{0,24},{32,38},{1,25},{33,39},{64,88},{96,102},{65,89},{97,103},{2... | collective-permute-start | bytes 2506760 | tf_op jit(solution)/shard_map/ppermute | solution.py:34
  35.4 21.1 %collective-permute-start.6 = (bf16[544,768]{1,0:T(8,128)(2,1)S(1)}, bf16[544,768]{1,0:T(8,128)(2,1)S(1)}, u32[]{:S(2)}, u32[]{:S(2)}) collective-permute-start(bf16[544,768]{1,0:T(8,128)(2,1)S(1)} %pad_maximum_fusion.1.refs_4_.refs_3_), channel_id=1, source_target_pairs={{0,2},{32,56},{1,3},{33,57},{64,66},{96,120},{65,67},{97,121},{2,0... | collective-permute-start | bytes 2506760 | tf_op jit(solution)/shard_map/ppermute | solution.py:34
  37.9 24.0 %collective-permute-start.5 = (bf16[544,768]{1,0:T(8,128)(2,1)S(1)}, bf16[544,768]{1,0:T(8,128)(2,1)S(1)}, u32[]{:S(2)}, u32[]{:S(2)}) collective-permute-start(bf16[544,768]{1,0:T(8,128)(2,1)S(1)} %pad_maximum_fusion.refs_3_.refs_2_), channel_id=1, source_target_pairs={{0,6},{32,40},{1,7},{33,41},{64,70},{96,104},{65,71},{97,105},{2,4... | collective-permute-start | bytes 2506760 | tf_op jit(solution)/shard_map/ppermute | solution.py:34
  38.1 23.9 %collective-permute-start.16 = (bf16[544,768]{1,0:T(8,128)(2,1)S(1)}, bf16[544,768]{1,0:T(8,128)(2,1)S(1)}, u32[]{:S(2)}, u32[]{:S(2)}) collective-permute-start(bf16[544,768]{1,0:T(8,128)(2,1)S(1)} %collective-permute-done.11.refs_5_.refs_4_), channel_id=1, source_target_pairs={{0,32},{32,0},{1,33},{33,1},{64,96},{96,64},{65,97},{97,65},{2,34}... | collective-permute-start | bytes 2506760 | tf_op jit(solution)/shard_map/ppermute | solution.py:34
  38.6 30.6 %collective-permute-start.12 = (bf16[544,768]{1,0:T(8,128)(2,1)S(1)}, bf16[544,768]{1,0:T(8,128)(2,1)S(1)}, u32[]{:S(2)}, u32[]{:S(2)}) collective-permute-start(bf16[544,768]{1,0:T(8,128)(2,1)S(1)} %collective-permute-done.11.refs_5_.refs_4_), channel_id=1, source_target_pairs={{0,2},{32,56},{1,3},{33,57},{64,66},{96,120},{65,67},{97,121},{2,0... | collective-permute-start | bytes 2506760 | tf_op jit(solution)/shard_map/ppermute | solution.py:34
  52.9 16.7 %collective-permute-start.10 = (bf16[544,768]{1,0:T(8,128)(2,1)S(1)}, bf16[544,768]{1,0:T(8,128)(2,1)S(1)}, u32[]{:S(2)}, u32[]{:S(2)}) collective-permute-start(bf16[544,768]{1,0:T(8,128)(2,1)S(1)} %collective-permute-done.9.refs_4_.refs_3_), channel_id=1, source_target_pairs={{0,6},{32,40},{1,7},{33,41},{64,70},{96,104},{65,71},{97,105},{2,4... | collective-permute-start | bytes 2506760 | tf_op jit(solution)/shard_map/ppermute | solution.py:34
  56.5 14.0 %collective-permute-start.15 = (bf16[544,768]{1,0:T(8,128)(2,1)S(1)}, bf16[544,768]{1,0:T(8,128)(2,1)S(1)}, u32[]{:S(2)}, u32[]{:S(2)}) collective-permute-start(bf16[544,768]{1,0:T(8,128)(2,1)S(1)} %collective-permute-done.9.refs_4_.refs_3_), channel_id=1, source_target_pairs={{0,32},{32,0},{1,33},{33,1},{64,96},{96,64},{65,97},{97,65},{2,34}... | collective-permute-start | bytes 2506760 | tf_op jit(solution)/shard_map/ppermute | solution.py:34
  61.9 15.6 %collective-permute-start.8 = (bf16[544,768]{1,0:T(8,128)(2,1)S(1)}, bf16[544,768]{1,0:T(8,128)(2,1)S(1)}, u32[]{:S(2)}, u32[]{:S(2)}) collective-permute-start(bf16[544,768]{1,0:T(8,128)(2,1)S(1)} %collective-permute-done.6.refs_5_.refs_4_), channel_id=1, source_target_pairs={{0,32},{32,0},{1,33},{33,1},{64,96},{96,64},{65,97},{97,65},{2,34}... | collective-permute-start | bytes 2506760 | tf_op jit(solution)/shard_map/ppermute | solution.py:34
  62.0 15.5 %collective-permute-start.7 = (bf16[544,768]{1,0:T(8,128)(2,1)S(1)}, bf16[544,768]{1,0:T(8,128)(2,1)S(1)}, u32[]{:S(2)}, u32[]{:S(2)}) collective-permute-start(bf16[544,768]{1,0:T(8,128)(2,1)S(1)} %collective-permute-done.5.refs_4_.refs_3_), channel_id=1, source_target_pairs={{0,32},{32,0},{1,33},{33,1},{64,96},{96,64},{65,97},{97,65},{2,34}... | collective-permute-start | bytes 2506760 | tf_op jit(solution)/shard_map/ppermute | solution.py:34
  69.2 17.2 %collective-permute-start.14 = (bf16[544,768]{1,0:T(8,128)(2,1)S(1)}, bf16[544,768]{1,0:T(8,128)(2,1)S(1)}, u32[]{:S(2)}, u32[]{:S(2)}) collective-permute-start(bf16[544,768]{1,0:T(8,128)(2,1)S(1)} %collective-permute-done.12.refs_9_.refs_5_.refs_4_), channel_id=1, source_target_pairs={{0,32},{32,0},{1,33},{33,1},{64,96},{96,64},{65,97},{97,65},{2,34}... | collective-permute-start | bytes 2506760 | tf_op jit(solution)/shard_map/ppermute | solution.py:34
  69.6 16.9 %collective-permute-start.13 = (bf16[544,768]{1,0:T(8,128)(2,1)S(1)}, bf16[544,768]{1,0:T(8,128)(2,1)S(1)}, u32[]{:S(2)}, u32[]{:S(2)}) collective-permute-start(bf16[544,768]{1,0:T(8,128)(2,1)S(1)} %collective-permute-done.10.refs_8_.refs_4_.refs_3_), channel_id=1, source_target_pairs={{0,32},{32,0},{1,33},{33,1},{64,96},{96,64},{65,97},{97,65},{2,34}... | collective-permute-start | bytes 2506760 | tf_op jit(solution)/shard_map/ppermute | solution.py:34
  87.9 8.2 %collective-permute-start.21 = (f16[256,768]{1,0:T(8,128)(2,1)S(1)}, f16[256,768]{1,0:T(8,128)(2,1)S(1)}, u32[]{:S(2)}, u32[]{:S(2)}) collective-permute-start(f16[256,768]{1,0:T(8,128)(2,1)S(1)} %multiply_convert_fusion.1), channel_id=1, source_target_pairs={{0,1},{32,97},{1,0},{33,96},{64,65},{96,33},{65,64},{97,32},{2,3},... | collective-permute-start | bytes 1179656 | tf_op jit(solution)/shard_map/ppermute | solution.py:34
  92.4 8.3 %collective-permute-start.19 = (f16[256,768]{1,0:T(8,128)(2,1)S(1)}, f16[256,768]{1,0:T(8,128)(2,1)S(1)}, u32[]{:S(2)}, u32[]{:S(2)}) collective-permute-start(f16[256,768]{1,0:T(8,128)(2,1)S(1)} %multiply_convert_fusion.2), channel_id=1, source_target_pairs={{0,1},{32,97},{1,0},{33,96},{64,65},{96,33},{65,64},{97,32},{2,3},... | collective-permute-start | bytes 1179656 | tf_op jit(solution)/shard_map/ppermute | solution.py:34
  96.2 7.8 %collective-permute-start.22 = (f16[256,768]{1,0:T(8,128)(2,1)S(1)}, f16[256,768]{1,0:T(8,128)(2,1)S(1)}, u32[]{:S(2)}, u32[]{:S(2)}) collective-permute-start(f16[256,768]{1,0:T(8,128)(2,1)S(1)} %multiply_convert_fusion), channel_id=1, source_target_pairs={{0,65},{32,33},{1,64},{33,32},{64,1},{96,97},{65,0},{97,96},{2,67}... | collective-permute-start | bytes 1179656 | tf_op jit(solution)/shard_map/ppermute | solution.py:34
